TPU v7x, 32 devices: a whole 2x2x4 slice. The times are simulated.
32 devices in a mesh: seq: 16 (over z, y, x), tp: 2 (over core).
Axes of the slice: x: 2, y: 2, z: 4, core: 2. Of those that a mesh axis runs over, the one named last changes fastest.
Arguments:
- query_rows: bfloat16 [2048, 2048], P('seq', 'tp'), may hold values from -350 to 350
- key_rows: bfloat16 [2048, 512], P('seq', 'tp'), may hold values from -6 to 6
- stored_value_rows: bfloat16 [2048, 512], P('seq', 'tp'), may hold values from -6 to 6
- output_grad: bfloat16 [2048, 2048], P('seq', 'tp'), may hold values from -96 to 96
- layer_input: bfloat16 [2048, 4096], P('seq', 'tp'), may hold values from -6 to 6
- key_matrix: bfloat16 [4096, 512], P(None, 'tp'), may hold values from -0.09375 to 0.09375
- value_matrix: bfloat16 [4096, 512], P(None, 'tp'), may hold values from -0.09375 to 0.09375
- run_placement: int32 [16, 16], replicated, may hold values from 0 to 15, as said below
Outputs:
- query_grad: bfloat16 [2048, 2048], P('seq', 'tp')
- input_grad: bfloat16 [2048, 4096], P('seq', 'tp')
- key_weight_grad: float32 [4096, 512], P('seq', 'tp')
- value_weight_grad: float32 [4096, 512], P('seq', 'tp')
Inputs may be any that keep to these rules, and one draw needn't show every extreme that they name: `run_placement`: row j gives, for each storing index d of seq, the slot within sequence block j of the 8 consecutive positions that d holds; every row is a permutation of 0 to 15.
All inputs are finite; a program needn't handle non-finite values.
Results may differ from a plain program's by a relative error of at most 0.0081.
Values may be sent and summed in bfloat16 or wider, within the bound.
A program may use at most 128 MiB of HBM per device.

v0:
```python
import math

import jax
import jax.numpy as jnp
from jax import lax
from jax.experimental import pallas as pl
from jax.experimental.pallas import tpu as pltpu
from jax.sharding import PartitionSpec as P

HEAD_SIZE = 128
WINDOW_LENGTH = 4096
GROUP = 4
CHUNK = 256
MASKED = -1e30
NT = (((1,), (1,)), ((), ()))
NN = (((1,), (0,)), ((), ()))
TN = (((0,), (0,)), ((), ()))
MESH = pl.DeviceIdType.MESH


def dot(a, b, dims):
    return lax.dot_general(a, b, dims, preferred_element_type=jnp.float32)


def flip(index, bit):
    return index + bit - 2 * bit * ((index // bit) % 2)


def bit_orders(count):
    bits = []
    while count > 1:
        count //= 2
        bits.append(count)
    return (bits[:-2] + bits[-2:][::-1], bits)


def step_kernel(
    q_ref, g_ref, k_ref, v_ref, qpos_ref, kpos_ref, x_ref, km_ref, vm_ref,
    dq_ref, all_ref, pair_ref, cols_ref, km_out, vm_out,
    kv_ref, part_ref, land_ref, s_ref,
    send_sem, recv_sem, x_send, x_recv, side_send, side_recv, local_sem,
):
    n = lax.axis_size("seq")
    me = lax.axis_index("seq")
    tp = lax.axis_index("tp")
    rows = q_ref.shape[0]
    keys = kv_ref.shape[0]
    kv_width = k_ref.shape[1]
    kv_local = kv_width // HEAD_SIZE
    features = x_ref.shape[1]
    half = n // 2
    x_width = cols_ref.shape[1]
    block_width = features // half
    orders = bit_orders(n)
    stages = len(orders[0])
    scale = 1.0 / math.sqrt(HEAD_SIZE)
    other = {"seq": me, "tp": 1 - tp}
    groups = []
    for c in range(kv_local):
        groups.append((slice(c * HEAD_SIZE, (c + 1) * HEAD_SIZE), orders[0]))
        groups.append((slice(kv_width + c * HEAD_SIZE, kv_width + (c + 1) * HEAD_SIZE), orders[1]))

    barrier = pltpu.get_barrier_semaphore()
    for step in range(1, n):
        pl.semaphore_signal(
            barrier, inc=1, device_id={"seq": (me + step) % n, "tp": tp}, device_id_type=MESH
        )
    pl.semaphore_signal(barrier, inc=1, device_id=other, device_id_type=MESH)
    pl.semaphore_wait(barrier, n)

    def block_of(order, ident):
        index = me
        for stage, bit in enumerate(order):
            if (ident >> stage) & 1:
                index = flip(index, bit)
        return index

    def span(index):
        return pl.ds(pl.multiple_of(index * rows, rows), rows)

    sent = []

    def send(phase, g, stage, ident, src, dst):
        copy = pltpu.make_async_remote_copy(
            src_ref=src,
            dst_ref=dst,
            send_sem=send_sem.at[phase, g, 2**stage + ident],
            recv_sem=recv_sem.at[phase, g, 2**stage + ident],
            device_id={"seq": flip(me, groups[g][1][stage]), "tp": tp},
            device_id_type=MESH,
        )
        copy.start()
        sent.append(copy)
        return copy

    def gather(phase, buffer, own):
        flying = {}

        def forward(g, ident, first):
            cols, order = groups[g]
            place = buffer.at[span(block_of(order, ident)), cols]
            src = own(g) if ident == 0 else place
            for stage in range(first, stages):
                flying[g, stage, ident] = send(phase, g, stage, ident, src, place)

        for g in range(len(groups)):
            forward(g, 0, 0)
        for stage in range(stages):
            for ident in range(2**stage):
                for g in range(len(groups)):
                    flying[g, stage, ident].wait_recv()
                    forward(g, 2**stage + ident, stage + 1)

    def own_input(g):
        cols = groups[g][0]
        if cols.start < kv_width:
            return k_ref.at[:, cols]
        return v_ref.at[:, slice(cols.start - kv_width, cols.stop - kv_width)]

    kv_ref[span(me), :kv_width] = k_ref[...]
    kv_ref[span(me), kv_width:] = v_ref[...]
    gather(0, kv_ref, own_input)

    side = []
    for i, (src, dst) in enumerate(((km_ref, km_out), (vm_ref, vm_out))):
        copy = pltpu.make_async_remote_copy(
            src_ref=src.at[pl.ds(pl.multiple_of((1 - tp) * features, features), features), :],
            dst_ref=dst,
            send_sem=side_send.at[i],
            recv_sem=side_recv.at[i],
            device_id=other,
            device_id_type=MESH,
        )
        copy.start()
        side.append(copy)

    def columns_of(target):
        start = ((target % half) * block_width) // x_width * x_width
        return x_ref.at[:, pl.ds(pl.multiple_of(start, x_width), x_width)]

    def x_copy(target, slot, source):
        return pltpu.make_async_remote_copy(
            src_ref=columns_of(target),
            dst_ref=cols_ref.at[span(me), :],
            send_sem=x_send.at[slot],
            recv_sem=x_recv.at[source],
            device_id={"seq": target, "tp": tp},
            device_id_type=MESH,
        )

    holder = tp == me // half
    own_columns = pltpu.make_async_copy(columns_of(me), cols_ref.at[span(me), :], local_sem)

    @pl.when(holder)
    def _():
        own_columns.start()

    for slot in range(half):
        target = tp * half + (me + slot) % half

        @pl.when(target != me)
        def _():
            x_copy(target, slot, me).start()

    qpos = jnp.concatenate([qpos_ref[...]] * GROUP, axis=1)
    wide = GROUP * rows
    chunks = keys // CHUNK
    moving = {}

    def reduce_send(g, stage, ident):
        cols, order = groups[g]
        moving[g, stage, ident] = send(
            1,
            g,
            stage,
            ident,
            part_ref.at[span(block_of(order, 2**stage + ident)), cols],
            land_ref.at[slice((2**stage + ident) * rows, (2**stage + ident + 1) * rows), cols],
        )

    for c in range(kv_local):
        first = c * GROUP
        heads = [slice((first + i) * HEAD_SIZE, (first + i + 1) * HEAD_SIZE) for i in range(GROUP)]
        q4 = jnp.concatenate([q_ref[:, h] for h in heads], axis=0)
        g4 = jnp.concatenate([g_ref[:, h] for h in heads], axis=0)
        k_cols = slice(c * HEAD_SIZE, (c + 1) * HEAD_SIZE)
        v_cols = slice(kv_width + c * HEAD_SIZE, kv_width + (c + 1) * HEAD_SIZE)

        def forward(i, carry):
            top, total, weighted = carry
            at = pl.ds(pl.multiple_of(i * CHUNK, CHUNK), CHUNK)
            kpos = kpos_ref[at, :]
            seen = (kpos <= qpos) & (kpos > qpos - WINDOW_LENGTH)
            s = jnp.where(seen, dot(kv_ref[at, k_cols], q4, NT) * scale, MASKED)
            dp = dot(kv_ref[at, v_cols], g4, NT)
            s_ref[at, :] = s
            new_top = jnp.maximum(top, jnp.max(s, axis=0, keepdims=True))
            e = jnp.exp(s - new_top)
            factor = jnp.exp(top - new_top)
            total = total * factor + jnp.sum(e, axis=0, keepdims=True)
            weighted = weighted * factor + jnp.sum(e * dp, axis=0, keepdims=True)
            return new_top, total, weighted

        zero = jnp.zeros((1, wide), jnp.float32)
        top, total, weighted = lax.fori_loop(
            0, chunks, forward, (jnp.full((1, wide), MASKED, jnp.float32), zero, zero)
        )
        lse = top + jnp.log(total)
        delta = weighted / total

        def backward(i, acc):
            at = pl.ds(pl.multiple_of(i * CHUNK, CHUNK), CHUNK)
            prob = jnp.exp(s_ref[at, :] - lse)
            dp = dot(kv_ref[at, v_cols], g4, NT)
            ds = (prob * (dp - delta)).astype(jnp.bfloat16)
            part_ref[at, k_cols] = (dot(ds, q4, NN) * scale).astype(jnp.bfloat16)
            part_ref[at, v_cols] = dot(prob.astype(jnp.bfloat16), g4, NN).astype(jnp.bfloat16)
            return acc + dot(kv_ref[at, k_cols], ds, TN)

        acc = lax.fori_loop(0, chunks, backward, jnp.zeros((HEAD_SIZE, wide), jnp.float32))
        dq = (jnp.transpose(acc) * scale).astype(jnp.bfloat16)
        for i, h in enumerate(heads):
            dq_ref[:, h] = dq[i * rows : (i + 1) * rows]
        for ident in range(2 ** (stages - 1)):
            for g in (2 * c, 2 * c + 1):
                reduce_send(g, stages - 1, ident)

    @pl.when(holder)
    def _():
        own_columns.wait()
        for step in range(1, n):
            x_copy(me, 0, (me + step) % n).wait_recv()

    relay = pltpu.make_async_remote_copy(
        src_ref=cols_ref,
        dst_ref=cols_ref,
        send_sem=side_send.at[2],
        recv_sem=side_recv.at[2],
        device_id=other,
        device_id_type=MESH,
    )

    @pl.when(holder)
    def _():
        relay.start()

    def add(g, stage, ident, out_ref):
        cols, order = groups[g]
        moving[g, stage, ident].wait_recv()
        at = span(block_of(order, ident))
        slot = 2**stage + ident
        landed = land_ref[slot * rows : (slot + 1) * rows, cols].astype(jnp.float32)
        out_ref[at, cols] = (part_ref[at, cols].astype(jnp.float32) + landed).astype(jnp.bfloat16)

    for stage in range(stages - 1, 0, -1):
        middle = 2 ** (stage - 1)
        for g in range(len(groups)):
            for ident in range(middle, 2 * middle):
                add(g, stage, ident, part_ref)
            for ident in range(middle):
                reduce_send(g, stage - 1, ident)
        for g in range(len(groups)):
            for ident in range(middle):
                add(g, stage, ident, part_ref)
    for g in range(len(groups)):
        add(g, 0, 0, all_ref)
    mate = pltpu.make_async_remote_copy(
        src_ref=all_ref.at[span(me), :],
        dst_ref=pair_ref,
        send_sem=side_send.at[3],
        recv_sem=side_recv.at[3],
        device_id=other,
        device_id_type=MESH,
    )
    mate.start()
    gather(2, all_ref, lambda g: all_ref.at[span(me), groups[g][0]])

    for copy in sent:
        copy.wait_send()
    for copy in side + [mate]:
        copy.wait()
    for slot in range(half):
        target = tp * half + (me + slot) % half

        @pl.when(target != me)
        def _():
            x_copy(target, slot, me).wait_send()

    @pl.when(holder)
    def _():
        relay.wait_send()

    @pl.when(tp != me // half)
    def _():
        relay.wait_recv()


def step(n, q, g, k, v, qpos, kpos, x, km, vm):
    rows, width = q.shape
    kv_width = k.shape[1]
    features = x.shape[1]
    keys = n * rows
    x_width = max(2 * features // n, 128)
    groups = 2 * kv_width // HEAD_SIZE
    vmem = pl.BlockSpec(memory_space=pltpu.VMEM)
    hbm = pl.BlockSpec(memory_space=pl.ANY)
    kind = jnp.bfloat16
    dma = pltpu.SemaphoreType.DMA
    return pl.pallas_call(
        step_kernel,
        out_shape=(
            jax.ShapeDtypeStruct((rows, width), kind),
            jax.ShapeDtypeStruct((keys, 2 * kv_width), kind),
            jax.ShapeDtypeStruct((rows, 2 * kv_width), kind),
            jax.ShapeDtypeStruct((keys, x_width), kind),
            jax.ShapeDtypeStruct((features, kv_width), kind),
            jax.ShapeDtypeStruct((features, kv_width), kind),
        ),
        in_specs=[vmem] * 6 + [hbm] * 3,
        out_specs=(vmem, vmem, vmem, hbm, hbm, hbm),
        scratch_shapes=[
            pltpu.VMEM((keys, 2 * kv_width), kind),
            pltpu.VMEM((keys, 2 * kv_width), kind),
            pltpu.VMEM((keys, 2 * kv_width), kind),
            pltpu.VMEM((keys, GROUP * rows), jnp.float32),
            dma((3, groups, n)),
            dma((3, groups, n)),
            dma((n // 2,)),
            dma((n,)),
            dma((4,)),
            dma((4,)),
            dma,
        ],
        compiler_params=pltpu.CompilerParams(
            vmem_limit_bytes=63 * 2**20, collective_id=0, has_side_effects=True
        ),
    )(q, g, k, v, qpos, kpos, x, km, vm)


def positions(run_placement, rows_here):
    seq_count = run_placement.shape[0]
    run_rows = rows_here // seq_count
    block = jnp.arange(seq_count, dtype=jnp.int32)[:, None] * rows_here
    start = jnp.transpose(block + run_placement * run_rows)
    return start[:, :, None] + jnp.arange(run_rows, dtype=jnp.int32)


def local(
    query_rows,
    key_rows,
    stored_value_rows,
    output_grad,
    layer_input,
    key_matrix,
    value_matrix,
    run_placement,
):
    seq_index = lax.axis_index("seq")
    rows_here = query_rows.shape[0]
    kv_width = key_rows.shape[1]
    pos = positions(run_placement, rows_here)
    kpos = pos.reshape(-1, 1)
    qpos = lax.dynamic_index_in_dim(pos, seq_index, 0, keepdims=False).reshape(1, rows_here)
    seq_count = run_placement.shape[0]
    query_grad, kv_all, kv_mate, columns, key_far, value_far = step(
        seq_count,
        query_rows,
        output_grad,
        key_rows,
        stored_value_rows,
        qpos,
        kpos,
        layer_input,
        key_matrix,
        value_matrix,
    )
    features = layer_input.shape[1]
    tp_index = lax.axis_index("tp")
    kv_grad = lax.dynamic_slice_in_dim(kv_all, seq_index * rows_here, rows_here, 0)
    key_near = lax.dynamic_slice_in_dim(key_matrix, tp_index * features, features, 0)
    value_near = lax.dynamic_slice_in_dim(value_matrix, tp_index * features, features, 0)
    input_grad = (
        dot(kv_grad[:, :kv_width], key_near, NT)
        + dot(kv_grad[:, kv_width:], value_near, NT)
        + dot(kv_mate[:, :kv_width], key_far, NT)
        + dot(kv_mate[:, kv_width:], value_far, NT)
    ).astype(jnp.bfloat16)
    block_width = 2 * features // seq_count
    shift = (seq_index * block_width) % columns.shape[1]
    columns = lax.dynamic_slice_in_dim(columns, shift, block_width, 1)
    key_weight = dot(columns, kv_all[:, :kv_width], TN)
    value_weight = dot(columns, kv_all[:, kv_width:], TN)
    return (query_grad, input_grad, key_weight, value_weight)


def solution(mesh):
    placed = (P("seq", "tp"),) * 5 + (P(None, "tp"), P(None, "tp"), P())
    return jax.shard_map(
        local,
        mesh=mesh,
        in_specs=placed,
        out_specs=(P("seq", "tp"),) * 4,
        check_vma=False,
    )
```

profile of v0, /device:TPU:0, one launch (start us, length us, event | category | flops | bytes accessed | tf_op | source)
XLA Modules:
  0.0 101.0 jit_solution(928874106085621939)
XLA Ops:
  0.6 0.8 add_bitcast_fusion
  1.4 0.1 copy.13
  1.5 0.1 iota_add_fusion
  1.6 0.6 reshape.41.qpos_ref
  2.2 1.3 %add.66.kpos_ref = s32[2048,1]{1,0:T(8,128)} reshape(s32[16,16,8]{2,1,0:T(8,128)S(1)} %iota_add_fusion) | data formatting | bytes 16384 | tf_op jit(solution)/shard_map/add | solution.py:345
  3.5 88.5 %shard_map.111 = (bf16[128,1024]{1,0:T(8,128)(2,1)}, bf16[2048,512]{1,0:T(8,128)(2,1)}, bf16[128,512]{1,0:T(8,128)(2,1)}, bf16[2048,256]{1,0:T(8,128)(2,1)}, bf1...) custom-call(bf16[128,1024]{1,0:T(8,128)(2,1)} %q_ref.1, bf16[128,1024]{1,0:T(8,128)(2,1)} %g_ref.1, ...), custom_call_target="tpu_custom_call" | custom-call | tf_op jit(solution)/shard_map/pallas_call | solution.py:309
  92.1 0.0 copy-start
  92.1 1.9 %fusion.6 = f32[128,2048]{1,0:T(8,128)S(1)} fusion(bf16[4096,256]{1,0:T(8,128)(2,1)} %km_ref.1, s32[]{:T(128)S(6)} %select_n.19, bf16[2048,512]{1,0:T(8,128)(2,1)} %get-tuple-element.11, s32[]{:T(128)S(6)} %select_n.18), kind=kOutput, calls=%fused_computation.9 | convolution fusion | flops 134217728 | bytes 2162696 | tf_op jit(solution)/shard_map/dot_general | solution.py:22
  94.0 0.0 copy-start.6
  94.0 0.0 copy-done
  94.0 0.0 copy-start.3
  94.0 1.4 %convolution_add_fusion.2 = f32[128,2048]{1,0:T(8,128)S(1)} fusion(f32[128,2048]{1,0:T(8,128)S(1)} %fusion.6, bf16[4096,256]{1,0:T(8,128)(2,1)S(1)} %copy-done, s32[]{:T(128)S(6)} %select_n.19, bf16[2048,512]{1,0:T(8,128)(2,1)} %get-tuple-element.11, s32[]{:T(128)S(6)} %select_n.18, s32[]{:T(128)S(6)} %add.67), kind=kOutput, calls=%fused_computation.2 | convolution fusion | flops 134479872 | bytes 3211276 | tf_op jit(solution)/shard_map/dot_general | solution.py:22
  95.4 0.0 copy-start.4
  95.4 0.0 copy-done.6
  95.4 0.0 copy-done.3
  95.5 0.0 copy-start.2
  95.5 0.5 convolution_add_fusion.1
  95.9 0.0 copy-start.1
  96.0 0.7 copy-done.4
  96.6 1.3 %fusion = bf16[128,2048]{1,0:T(8,128)(2,1)} fusion(f32[128,2048]{1,0:T(8,128)S(1)} %convolution_add_fusion.1, bf16[2048,256]{1,0:T(8,128)(2,1)S(1)} %copy-done.4, bf16[128,512]{1,0:T(8,128)(2,1)S(1)} %copy-done.6), kind=kOutput, calls=%fused_computation.3 | convolution fusion | flops 134742016 | bytes 2686976 | tf_op jit(solution)/shard_map/dot_general | solution.py:22
  97.9 0.0 copy-done.2
  97.9 0.0 copy-done.1
  97.9 0.0 copy-start.5
  97.9 1.2 %fusion.1 = f32[256,256]{1,0:T(8,128)} fusion(bf16[2048,256]{1,0:T(8,128)(2,1)S(1)} %copy-done.1, bf16[2048,512]{1,0:T(8,128)(2,1)S(1)} %copy-done.2), kind=kOutput, calls=%fused_computation.4 | convolution fusion | flops 268435456 | bytes 2359296 | tf_op jit(solution)/shard_map/dot_general | solution.py:22
  99.1 1.2 %fusion.3 = f32[256,256]{1,0:T(8,128)} fusion(bf16[2048,256]{1,0:T(8,128)(2,1)S(1)} %copy-done.1, bf16[2048,512]{1,0:T(8,128)(2,1)S(1)} %copy-done.2), kind=kOutput, calls=%fused_computation.6 | convolution fusion | flops 268435456 | bytes 2359296 | tf_op jit(solution)/shard_map/dot_general | solution.py:22
  100.3 0.0 copy-done.5
  100.3 0.7 copy.16
  (2 shorter events, 0.0 us)
Async XLA Ops:
  92.1 1.9 %copy-start = (bf16[4096,256]{1,0:T(8,128)(2,1)S(1)}, bf16[4096,256]{1,0:T(8,128)(2,1)}, u32[]{:S(2)}) copy-start(bf16[4096,256]{1,0:T(8,128)(2,1)} %vm_ref.1) | copy-start | bytes 6291460
  94.0 1.5 %copy-start.6 = (bf16[128,512]{1,0:T(8,128)(2,1)S(1)}, bf16[128,512]{1,0:T(8,128)(2,1)}, u32[]{:S(2)}) copy-start(bf16[128,512]{1,0:T(8,128)(2,1)} %get-tuple-element.12) | copy-start | bytes 393220
  94.0 1.4 %copy-start.3 = (bf16[2048,256]{1,0:T(8,128)(2,1)S(1)}, bf16[2048,256]{1,0:T(8,128)(2,1)}, u32[]{:S(2)}) copy-start(bf16[2048,256]{1,0:T(8,128)(2,1)} %get-tuple-element.13) | copy-start | bytes 3145732
  95.4 1.2 %copy-start.4 = (bf16[2048,256]{1,0:T(8,128)(2,1)S(1)}, bf16[2048,256]{1,0:T(8,128)(2,1)}, u32[]{:S(2)}) copy-start(bf16[2048,256]{1,0:T(8,128)(2,1)} %get-tuple-element.14) | copy-start | bytes 3145732
  95.5 2.5 %copy-start.2 = (bf16[2048,512]{1,0:T(8,128)(2,1)S(1)}, bf16[2048,512]{1,0:T(8,128)(2,1)}, u32[]{:S(2)}) copy-start(bf16[2048,512]{1,0:T(8,128)(2,1)} %get-tuple-element.11) | copy-start | bytes 6291460
  95.9 2.0 %copy-start.1 = (bf16[2048,256]{1,0:T(8,128)(2,1)S(1)}, bf16[2048,256]{1,0:T(8,128)(2,1)}, u32[]{:S(2)}) copy-start(bf16[2048,256]{1,0:T(8,128)(2,1)} %get-tuple-element.15) | copy-start | bytes 3145732
  97.9 2.4 %copy-start.5 = (bf16[128,1024]{1,0:T(8,128)(2,1)S(1)}, bf16[128,1024]{1,0:T(8,128)(2,1)}, u32[]{:S(2)}) copy-start(bf16[128,1024]{1,0:T(8,128)(2,1)} %get-tuple-element.20) | copy-start | bytes 786436
where the time goes:
time: 101 us
  Pallas kernels  88.5 us (88%)
  matrix products  7.37 us (7%)
  local copies, waits for them, and re-layouts  3.44 us (3%)
    pallas_call x1, Pallas kernels, step(): pl.pallas_call(step_kernel, out_shape=(jax.ShapeDtypeStruct((rows, width)...  88.5 us
    dot_general x6, matrix products, dot(): return lax.dot_general(a, b, dims, preferred_element_type=jnp.float32)  7.37 us

commit v1 on v0

v1 whole, which is shorter than its diff:
```python
import math

import jax
import jax.numpy as jnp
from jax import lax
from jax.experimental import pallas as pl
from jax.experimental.pallas import tpu as pltpu
from jax.sharding import PartitionSpec as P

HEAD_SIZE = 128
WINDOW_LENGTH = 4096
GROUP = 4
CHUNK = 512
MASKED = -1e30
NT = (((1,), (1,)), ((), ()))
NN = (((1,), (0,)), ((), ()))
TN = (((0,), (0,)), ((), ()))
MESH = pl.DeviceIdType.MESH


def dot(a, b, dims):
    return lax.dot_general(a, b, dims, preferred_element_type=jnp.float32)


def flip(index, bit):
    return index + bit - 2 * bit * ((index // bit) % 2)


def step_kernel(
    q_ref, g_ref, k_ref, v_ref, pos_ref, x_ref, km_ref, vm_ref,
    dq_ref, own_ref, pair_ref, kw_ref, vw_ref, km_out, vm_out,
    kv_ref, qb_ref, gb_ref, kpos_ref, s_ref, dp_ref, p_ref, ds_ref, dqb_ref, dqa_ref,
    sum_ref, give_ref, take_ref, zs_ref, land_ref, fin_ref, all_ref, cols_ref, acc_ref,
    plane_send, kv_recv, kvz_send, kvp_send, kvp_recv, qg_send, qg_recv,
    x_send, x_recv, side_send, side_recv, local_sem,
    give_send, give_recv, z_send, z_recv, col_send, ag_send, ag_recv, dq_send, dq_recv,
):
    n = lax.axis_size("seq")
    cores = lax.axis_size("tp")
    me = lax.axis_index("seq")
    tp = lax.axis_index("tp")
    parts, run, _ = q_ref.shape
    kv_local = k_ref.shape[2] // HEAD_SIZE
    plane = cores * kv_local
    pair = GROUP // cores
    depth = n // plane
    z = me // plane
    p = me % plane
    home = p // kv_local
    lane = p % kv_local
    block = plane * run
    keys = n * run
    wide = pair * block
    sub = min(keys, CHUNK)
    roomy = dp_ref.shape[0] > 1
    windowed = parts * keys > WINDOW_LENGTH
    features = x_ref.shape[2]
    half = n // cores
    x_width = cols_ref.shape[2]
    block_width = features // half
    scale = 1.0 / math.sqrt(HEAD_SIZE)
    power = scale * math.log2(math.e)
    other = {"seq": me, "tp": 1 - tp}

    barrier = pltpu.get_barrier_semaphore()
    for step in range(n):
        for core in range(cores):
            if step or core:
                pl.semaphore_signal(
                    barrier,
                    inc=1,
                    device_id={"seq": (me + step) % n, "tp": (tp + core) % cores},
                    device_id_type=MESH,
                )
    pl.semaphore_wait(barrier, n * cores - 1)

    sent = []

    def when(cond, action):
        if cond is None:
            action()
        else:
            pl.when(cond)(action)

    def send(src, dst, send_sem, recv_sem, device, cond=None):
        def copy():
            return pltpu.make_async_remote_copy(
                src_ref=src, dst_ref=dst, send_sem=send_sem, recv_sem=recv_sem,
                device_id=device, device_id_type=MESH,
            )

        when(cond, lambda: copy().start())
        sent.append((cond, lambda: copy().wait_send()))

    def arrive(dst, recv_sem, cond=None):
        def wait():
            pltpu.make_async_remote_copy(
                src_ref=dst, dst_ref=dst, send_sem=recv_sem, recv_sem=recv_sem,
                device_id=other, device_id_type=MESH,
            ).wait_recv()

        when(cond, wait)

    def rows_of(index, count):
        return pl.ds(pl.multiple_of(index * count, count), count)

    def lanes_of(index):
        return pl.ds(pl.multiple_of(index * HEAD_SIZE, HEAD_SIZE), HEAD_SIZE)

    def piece(role, source):
        return kv_ref.at[role, :, rows_of(source, run), :]

    for i in range(kv_local):
        head = tp * kv_local + i
        target = z * plane + head
        for role, ref in enumerate((k_ref, v_ref)):
            mine = (head == p) & (tp == role)
            cols = slice(i * HEAD_SIZE, (i + 1) * HEAD_SIZE)
            send(
                ref.at[:, :, cols], piece(role, me), plane_send.at[i, role], kv_recv.at[me],
                {"seq": target, "tp": role}, jnp.logical_not(mine),
            )

            @pl.when(mine)
            def _():
                kv_ref[role, :, rows_of(me, run), :] = ref[:, :, cols]

    for i in range(kv_local):
        head = tp * kv_local + i
        target = z * plane + head
        for u in range(cores):
            mine = (head == p) & (tp == u)
            for h in range(pair):
                first = (i * GROUP + u * pair + h) * HEAD_SIZE
                cols = slice(first, first + HEAD_SIZE)
                for w, (ref, buf) in enumerate(((q_ref, qb_ref), (g_ref, gb_ref))):
                    send(
                        ref.at[:, :, cols], buf.at[:, h, rows_of(p, run), :],
                        qg_send.at[w, i, u, h], qg_recv.at[w, p, h],
                        {"seq": target, "tp": u}, jnp.logical_not(mine),
                    )

                    @pl.when(mine)
                    def _():
                        buf[:, h, rows_of(p, run), :] = ref[:, :, cols]

    pos_t = jnp.transpose(pos_ref[...])
    for b in range(parts):
        for s in range(depth):
            column = pos_t[:, s * parts + b : s * parts + b + 1]
            kpos_ref[b, s * block : (s + 1) * block, :] = jnp.broadcast_to(column, (block, block))

    def both(source):
        place = piece(tp, source)
        send(place, place, kvz_send.at[0, source], kv_recv.at[source],
             {"seq": jnp.minimum(me + plane, n - 1), "tp": tp}, z + 1 < depth)
        send(place, place, kvz_send.at[1, source], kv_recv.at[source],
             {"seq": jnp.maximum(me - plane, 0), "tp": tp}, z > 0)
        send(place, place, kvp_send.at[source], kvp_recv.at[source], other)

    for j in range(plane):
        index = (p + j) % plane
        source = z * plane + index
        if j == 0:
            arrive(piece(tp, source), kv_recv.at[source], home != tp)
        else:
            arrive(piece(tp, source), kv_recv.at[source])
        both(source)

    for k in range(1, depth):
        for j in range(plane):
            index = (p + j) % plane
            for way in range(2):
                at = z - k if way == 0 else z + k
                valid = at >= 0 if way == 0 else at < depth
                onward = valid & (z + 1 < depth) if way == 0 else valid & (z > 0)
                source = jnp.clip(at, 0, depth - 1) * plane + index
                place = piece(tp, source)
                arrive(place, kv_recv.at[source], valid)
                to = jnp.minimum(me + plane, n - 1) if way == 0 else jnp.maximum(me - plane, 0)
                send(place, place, kvz_send.at[way, source], kv_recv.at[source],
                     {"seq": to, "tp": tp}, onward)
                send(place, place, kvp_send.at[source], kvp_recv.at[source], other, valid)

    for w, buf in enumerate((qb_ref, gb_ref)):
        for j in range(plane):
            for h in range(pair):
                here = (p == j) & (home == tp)
                arrive(buf.at[:, h, j * run : (j + 1) * run, :], qg_recv.at[w, j, h],
                       jnp.logical_not(here))

    for i, (src, dst) in enumerate(((km_ref, km_out), (vm_ref, vm_out))):
        send(
            src.at[pl.ds(pl.multiple_of((1 - tp) * features, features), features), :], dst,
            side_send.at[i], side_recv.at[i], other,
        )

    def columns_of(target):
        start = ((target % half) * block_width) // x_width * x_width
        return x_ref.at[:, :, pl.ds(pl.multiple_of(start, x_width), x_width)]

    holder = tp == me // half
    own_columns = pltpu.make_async_copy(
        columns_of(me), cols_ref.at[:, rows_of(me, run), :], local_sem
    )

    @pl.when(holder)
    def _():
        own_columns.start()

    for slot in range(half):
        target = tp * half + (me + slot) % half
        send(
            columns_of(target), cols_ref.at[:, rows_of(me, run), :],
            x_send.at[slot], x_recv.at[me], {"seq": target, "tp": tp}, target != me,
        )

    for source in range(n):
        arrive(kv_ref.at[1 - tp, :, source * run : (source + 1) * run, :], kvp_recv.at[source])

    def lowest(a):
        low = 0
        while windowed and (a - low - 1) * keys + 1 >= WINDOW_LENGTH:
            low += 1
        return low

    tiles = [(a, b) for a in range(parts) for b in range(lowest(a), a + 1)]
    where = {tile: t for t, tile in enumerate(tiles)}

    def sweep(body, carry):
        if keys == sub:
            return body(slice(0, keys), carry)
        return lax.fori_loop(0, keys // sub, lambda i, c: body(rows_of(i, sub), c), carry)

    inverse, delta = [], []
    for a in range(parts):
        qa = qb_ref[a].reshape(wide, HEAD_SIZE)
        ga = gb_ref[a].reshape(wide, HEAD_SIZE)
        qpos = pos_ref[pl.ds(z * parts + a, 1), :]
        lows = range(lowest(a), a + 1)
        top = jnp.full((1, wide), MASKED, jnp.float32)
        for b in lows:

            def scores(at, top):
                s = dot(kv_ref[0, b, at, :], qa, NT)
                if a == b or windowed:
                    kpos = kpos_ref[b, at, :]
                    seen = kpos <= qpos
                    if windowed:
                        seen = seen & (kpos > qpos - WINDOW_LENGTH)
                    s = jnp.concatenate(
                        [
                            jnp.where(seen, s[:, h * block : (h + 1) * block], MASKED)
                            for h in range(pair)
                        ],
                        axis=1,
                    )
                s_ref[where[a, b], at, :] = s
                return jnp.maximum(top, jnp.max(s, axis=0, keepdims=True))

            top = sweep(scores, top)
        carry = (jnp.zeros((1, wide), jnp.float32), jnp.zeros((1, wide), jnp.float32))
        for b in lows:

            def sums(at, carry):
                total, weighted = carry
                e = jnp.exp2((s_ref[where[a, b], at, :] - top) * power)
                dp = dot(kv_ref[1, b, at, :], ga, NT)
                s_ref[where[a, b], at, :] = e
                if roomy:
                    dp_ref[where[a, b], at, :] = dp
                return (
                    total + jnp.sum(e, axis=0, keepdims=True),
                    weighted + jnp.sum(e * dp, axis=0, keepdims=True),
                )

            carry = sweep(sums, carry)
        total, weighted = carry
        inverse.append(1.0 / total)
        delta.append(weighted / total)

    def backward(b):
        uppers = [a for a in range(parts) if (a, b) in where]
        lo, hi = uppers[0], uppers[-1] + 1
        d = b if roomy else 0
        for a in uppers:
            lanes = slice(a * wide, (a + 1) * wide)

            def grads(at, carry):
                prob = s_ref[where[a, b], at, :] * inverse[a]
                if roomy:
                    dp = dp_ref[where[a, b], at, :]
                else:
                    dp = dot(kv_ref[1, b, at, :], gb_ref[a].reshape(wide, HEAD_SIZE), NT)
                p_ref[at, lanes] = prob.astype(jnp.bfloat16)
                ds_ref[d, at, lanes] = (prob * (dp - delta[a])).astype(jnp.bfloat16)
                return carry

            sweep(grads, 0)
        lanes = slice(lo * wide, hi * wide)
        q_all = qb_ref[lo:hi].reshape((hi - lo) * wide, HEAD_SIZE)
        g_all = gb_ref[lo:hi].reshape((hi - lo) * wide, HEAD_SIZE)

        def products(at, carry):
            dk = dot(ds_ref[d, at, lanes], q_all, NN) * scale
            dv = dot(p_ref[at, lanes], g_all, NN)
            first = tp == 0
            sum_ref[b, at, :] = jnp.where(first, dk, dv)
            give_ref[b, at, :] = jnp.where(first, dv, dk).astype(jnp.bfloat16)
            return carry

        sweep(products, 0)
        send(give_ref.at[b], take_ref.at[b], give_send.at[b], give_recv.at[b], other)
        if not roomy:
            for a in uppers:
                query_sum(a, b)

    def query_sum(a, b):
        d = b if roomy else 0
        lanes = slice(a * wide, (a + 1) * wide)

        def add(at, acc):
            return acc + dot(kv_ref[0, b, at, :], ds_ref[d, at, lanes], TN)

        acc = sweep(add, jnp.zeros((HEAD_SIZE, wide), jnp.float32))
        if b == a:
            dqa_ref[a] = acc
        else:
            dqa_ref[a] += acc

    def cross(b):
        arrive(take_ref.at[b], give_recv.at[b])
        total = sum_ref[b] + take_ref[b].astype(jnp.float32)
        sum_ref[b] = total
        zs_ref[b] = total.astype(jnp.bfloat16)
        for k in range(1, depth):
            to = (z + k) % depth
            send(
                zs_ref.at[b, rows_of(to, block), :], land_ref.at[b, k],
                z_send.at[b, k], z_recv.at[b, k], {"seq": to * plane + p, "tp": tp},
            )

    out_col = tp * kv_local + lane

    def finish(b):
        total = sum_ref[b, rows_of(z, block), :]
        for k in range(1, depth):
            arrive(land_ref.at[b, k], z_recv.at[b, k])
            total = total + land_ref[b, k].astype(jnp.float32)
        fin_ref[b] = total.astype(jnp.bfloat16)
        place = all_ref.at[b, out_col, rows_of(z, block), :]
        slot = ag_recv.at[b, z, out_col]
        send(fin_ref.at[b], place, col_send.at[b, 0], slot, other, home != tp)
        for k in range(1, depth):
            to = (z + k) % depth
            send(fin_ref.at[b], place, col_send.at[b, k], slot, {"seq": to * plane + p, "tp": home})

        @pl.when(home == tp)
        def _():
            all_ref[b, out_col, rows_of(z, block), :] = fin_ref[b]

    owner = home == tp
    mate_lane = kv_local - 1 - lane
    near = {"seq": z * plane + flip(p, 1), "tp": tp}
    across = {"seq": z * plane + flip(p, 2), "tp": tp}

    def gathered(b, at, c):
        return all_ref.at[b, c, rows_of(at, block), :], ag_recv.at[b, at, c]

    def push(b):
        for k in range(depth):
            at = (z + k) % depth
            for role in range(cores):
                c = role * kv_local + lane
                place, slot = gathered(b, at, c)
                arrive(place, slot, owner & (tp != role) if k == 0 else owner)
                send(place, place, ag_send.at[b, at, c, 0], slot, near, owner)
                send(place, place, ag_send.at[b, at, c, 1], slot, across, owner)

    def relay(b):
        for k in range(depth):
            at = (z + k) % depth
            c = mate_lane
            place, slot = gathered(b, at, c)
            arrive(place, slot, owner)
            send(place, place, ag_send.at[b, at, c, 1], slot, across, owner)
            c = kv_local + lane
            place, slot = gathered(b, at, c)
            arrive(place, slot, jnp.logical_not(owner))
            send(place, place, ag_send.at[b, at, c, 0], slot, near, jnp.logical_not(owner))

    def collect(b):
        for k in range(depth):
            at = (z + k) % depth
            place, slot = gathered(b, at, kv_local + mate_lane)
            arrive(place, slot)
            for c in (lane, mate_lane):
                place, slot = gathered(b, at, c)
                arrive(place, slot, jnp.logical_not(owner))

    def weigh(b, first):
        grads = [all_ref[b, c] for c in range(cores * kv_local)]
        part = dot(cols_ref[b], jnp.concatenate(grads, axis=1), TN)
        if first:
            acc_ref[...] = part
        else:
            acc_ref[...] += part

    def columns():
        @pl.when(holder)
        def _():
            own_columns.wait()

        for step in range(1, n):
            source = (me + step) % n
            arrive(cols_ref.at[:, rows_of(source, run), :], x_recv.at[source], holder)
        send(cols_ref, cols_ref, side_send.at[2], side_recv.at[2], other, holder)
        arrive(cols_ref, side_recv.at[2], jnp.logical_not(holder))

    def queries():
        for a in range(parts):
            if roomy:
                for b in reversed(range(lowest(a), a + 1)):
                    query_sum(a, b)
            out = (jnp.transpose(dqa_ref[a]) * scale).astype(jnp.bfloat16)
            dqb_ref[a] = out.reshape(pair, block, HEAD_SIZE)
        for j in range(plane):
            for h in range(pair):
                cols = lanes_of(lane * GROUP + tp * pair + h)
                mine = (p == j) & (home == tp)
                src = dqb_ref.at[:, h, j * run : (j + 1) * run, :]
                send(
                    src, dq_ref.at[:, :, cols], dq_send.at[h, j], dq_recv.at[lane, tp, h],
                    {"seq": z * plane + j, "tp": home}, jnp.logical_not(mine),
                )

                @pl.when(mine)
                def _():
                    dq_ref[:, :, cols] = dqb_ref[:, h, j * run : (j + 1) * run, :]

    last = parts - 1
    for tick in range(parts + 2):
        for level, stage in enumerate((backward, cross, finish)):
            b = last - (tick - level)
            if 0 <= b <= last:
                stage(b)
        if tick >= 2:
            push(last - (tick - 2))
        if tick == parts - 1:
            queries()
    for b in reversed(range(parts)):
        relay(b)
    columns()
    for b in reversed(range(parts)):
        collect(b)
        weigh(b, b == last)

    own_rows = rows_of(me, run)
    send(all_ref.at[:, :, own_rows, :], pair_ref, side_send.at[3], side_recv.at[3], other)
    own_ref[...] = all_ref[:, :, own_rows, :]
    middle = kv_local * HEAD_SIZE
    kw_ref[...] = acc_ref[:, :middle]
    vw_ref[...] = acc_ref[:, middle:]

    for i in range(kv_local):
        for u in range(cores):
            for h in range(pair):
                first = (i * GROUP + u * pair + h) * HEAD_SIZE
                here = (p == tp * kv_local + i) & (tp == u)
                arrive(dq_ref.at[:, :, first : first + HEAD_SIZE], dq_recv.at[i, u, h],
                       jnp.logical_not(here))
    for i, dst in enumerate((km_out, vm_out)):
        arrive(dst, side_recv.at[i])
    arrive(pair_ref, side_recv.at[3])
    for cond, wait in sent:
        when(cond, wait)


def step(n, q, g, k, v, pos, x, km, vm):
    parts, run, width = q.shape
    kv_width = k.shape[2]
    kv_local = kv_width // HEAD_SIZE
    features = x.shape[2]
    heads = width // HEAD_SIZE
    cores = km.shape[0] // features
    plane = cores * kv_local
    pair = GROUP // cores
    depth = n // plane
    block = plane * run
    keys = n * run
    wide = pair * block
    x_width = max(cores * features // n, 128)
    roomy = parts * keys <= 4096
    tiles = parts * (parts + 1) // 2
    vmem = pl.BlockSpec(memory_space=pltpu.VMEM)
    hbm = pl.BlockSpec(memory_space=pl.ANY)
    kind = jnp.bfloat16
    real = jnp.float32
    dma = pltpu.SemaphoreType.DMA
    return pl.pallas_call(
        step_kernel,
        out_shape=(
            jax.ShapeDtypeStruct((parts, run, width), kind),
            jax.ShapeDtypeStruct((parts, 2 * kv_local, run, HEAD_SIZE), kind),
            jax.ShapeDtypeStruct((parts, 2 * kv_local, run, HEAD_SIZE), kind),
            jax.ShapeDtypeStruct((x_width, kv_width), real),
            jax.ShapeDtypeStruct((x_width, kv_width), real),
            jax.ShapeDtypeStruct((features, kv_width), kind),
            jax.ShapeDtypeStruct((features, kv_width), kind),
        ),
        in_specs=[vmem] * 5 + [hbm] * 3,
        out_specs=(vmem, vmem, vmem, vmem, vmem, hbm, hbm),
        scratch_shapes=[
            pltpu.VMEM((2, parts, keys, HEAD_SIZE), kind),
            pltpu.VMEM((parts, pair, block, HEAD_SIZE), kind),
            pltpu.VMEM((parts, pair, block, HEAD_SIZE), kind),
            pltpu.VMEM((parts, keys, block), real),
            pltpu.VMEM((tiles, keys, wide), real),
            pltpu.VMEM((tiles, keys, wide) if roomy else (1, 8, 128), real),
            pltpu.VMEM((keys, parts * wide), kind),
            pltpu.VMEM((parts if roomy else 1, keys, parts * wide), kind),
            pltpu.VMEM((parts, pair, block, HEAD_SIZE), kind),
            pltpu.VMEM((parts, HEAD_SIZE, wide), real),
            pltpu.VMEM((parts, keys, HEAD_SIZE), real),
            pltpu.VMEM((parts, keys, HEAD_SIZE), kind),
            pltpu.VMEM((parts, keys, HEAD_SIZE), kind),
            pltpu.VMEM((parts, keys, HEAD_SIZE), kind),
            pltpu.VMEM((parts, depth, block, HEAD_SIZE), kind),
            pltpu.VMEM((parts, block, HEAD_SIZE), kind),
            pltpu.VMEM((parts, 2 * kv_local, keys, HEAD_SIZE), kind),
            pltpu.VMEM((parts, keys, x_width), kind),
            pltpu.VMEM((x_width, 2 * kv_width), real),
            dma((kv_local, cores)),
            dma((n,)),
            dma((2, n)),
            dma((n,)),
            dma((n,)),
            dma((2, kv_local, cores, pair)),
            dma((2, plane, pair)),
            dma((n // cores,)),
            dma((n,)),
            dma((4,)),
            dma((4,)),
            dma,
            dma((parts,)),
            dma((parts,)),
            dma((parts, depth)),
            dma((parts, depth)),
            dma((parts, depth)),
            dma((parts, depth, cores * kv_local, 2)),
            dma((parts, depth, cores * kv_local)),
            dma((pair, plane)),
            dma((kv_local, cores, pair)),
        ],
        compiler_params=pltpu.CompilerParams(
            vmem_limit_bytes=63 * 2**20, collective_id=0, has_side_effects=True
        ),
    )(q, g, k, v, pos, x, km, vm)


def positions(run_placement, rows_here, parts):
    seq_count = run_placement.shape[0]
    run_rows = rows_here // seq_count
    block = jnp.arange(seq_count, dtype=jnp.int32)[:, None] * rows_here
    start = jnp.transpose(block + run_placement * run_rows)
    pos = start[:, :, None] + jnp.arange(run_rows, dtype=jnp.int32)
    plane = parts
    pos = pos.reshape(seq_count // plane, plane, parts, rows_here // parts)
    pos = jnp.transpose(pos, (0, 2, 1, 3)).reshape(seq_count, rows_here)
    return pos.astype(jnp.float32)


def local(
    query_rows,
    key_rows,
    stored_value_rows,
    output_grad,
    layer_input,
    key_matrix,
    value_matrix,
    run_placement,
):
    seq_index = lax.axis_index("seq")
    tp_index = lax.axis_index("tp")
    seq_count = run_placement.shape[0]
    rows_here = query_rows.shape[0]
    kv_width = key_rows.shape[1]
    features = layer_input.shape[1]
    parts = (key_matrix.shape[0] // features) * (kv_width // HEAD_SIZE)

    def cut(array):
        return array.reshape(parts, rows_here // parts, array.shape[1])

    query_grad, kv_grad, kv_mate, key_weight, value_weight, key_far, value_far = step(
        seq_count,
        cut(query_rows),
        cut(output_grad),
        cut(key_rows),
        cut(stored_value_rows),
        positions(run_placement, rows_here, parts),
        cut(layer_input),
        key_matrix,
        value_matrix,
    )
    kv_grad = jnp.swapaxes(kv_grad, 1, 2).reshape(rows_here, 2 * kv_width)
    kv_mate = jnp.swapaxes(kv_mate, 1, 2).reshape(rows_here, 2 * kv_width)
    key_near = lax.dynamic_slice_in_dim(key_matrix, tp_index * features, features, 0)
    value_near = lax.dynamic_slice_in_dim(value_matrix, tp_index * features, features, 0)
    input_grad = (
        dot(kv_grad[:, :kv_width], key_near, NT)
        + dot(kv_grad[:, kv_width:], value_near, NT)
        + dot(kv_mate[:, :kv_width], key_far, NT)
        + dot(kv_mate[:, kv_width:], value_far, NT)
    ).astype(jnp.bfloat16)
    block_width = 2 * features // seq_count
    if key_weight.shape[0] != block_width:
        shift = (seq_index * block_width) % key_weight.shape[0]
        key_weight = lax.dynamic_slice_in_dim(key_weight, shift, block_width, 0)
        value_weight = lax.dynamic_slice_in_dim(value_weight, shift, block_width, 0)
    return (query_grad.reshape(query_rows.shape), input_grad, key_weight, value_weight)


def solution(mesh):
    placed = (P("seq", "tp"),) * 5 + (P(None, "tp"), P(None, "tp"), P())
    return jax.shard_map(
        local,
        mesh=mesh,
        in_specs=placed,
        out_specs=(P("seq", "tp"),) * 4,
        check_vma=False,
    )
```

time: 101 us -> 89.7 us (0.89); the launches traced: 101 us -> 88.4 us
  Pallas kernels: 88.5 us -> 76.2 us
  matrix products: 7.37 us -> 3.94 us
  local copies, waits for them, and re-layouts: 3.44 us -> 6.77 us
    pallas_call x1, Pallas kernels: 88.5 us -> 76.2 us  [step(): pl.pallas_call(step_kernel, out_shape=(jax.ShapeDtypeStruct((parts, run,...]
    dot_general x6 -> x4, matrix products: 7.37 us -> 3.94 us  [dot(): return lax.dot_general(a, b, dims, preferred_element_type=jnp.float32)]
    unnamed x15 -> x17, local copies, waits for them, and re-layouts: 1.45 us -> 3.64 us
    transpose x0 -> x2, local copies, waits for them, and re-layouts: none -> 2.1 us  [the longest x1 1.12 us: local(): kv_grad = jnp.swapaxes(kv_grad, 1, 2).reshape(rows_here, 2 * kv_width)]
    add x1 -> x4, local copies, waits for them, and re-layouts: 1.3 us -> 0.28 us  [positions(): pos = start[:, :, None] + jnp.arange(run_rows, dtype=jnp.int32)]
where the time goes in v1:
time: 89.7 us; the launch traced here: 88.4 us
  Pallas kernels  76.2 us (85%)
  local copies, waits for them, and re-layouts  6.77 us (8%)
  matrix products  3.94 us (4%)
    pallas_call x1, Pallas kernels, step(): pl.pallas_call(step_kernel, out_shape=(jax.ShapeDtypeStruct((parts, run,...  76.2 us
    dot_general x4, matrix products, dot(): return lax.dot_general(a, b, dims, preferred_element_type=jnp.float32)  3.94 us
    unnamed x17, local copies, waits for them, and re-layouts  3.64 us

profile of v1, /device:TPU:0, one launch (start us, length us, event | category | flops | bytes accessed | tf_op | source)
XLA Modules:
  0.0 88.4 jit_solution(3449728654216790717)
XLA Ops:
  0.7 0.1 add.46
  0.7 0.8 add_bitcast_fusion
  1.5 0.1 copy.13
  1.6 0.1 add.43
  1.7 0.1 add.44
  1.8 0.7 convert_element_type.12.pos_ref
  2.5 76.2 %shard_map.111 = (bf16[4,32,1024]{2,1,0:T(8,128)(2,1)}, bf16[4,4,32,128]{3,2,1,0:T(8,128)(2,1)}, bf16[4,4,32,128]{3,2,1,0:T(8,128)(2,1)}, f32[256,256]{1,0:T(8,1...) custom-call(bf16[4,32,1024]{2,1,0:T(8,128)(2,1)} %bitcast.32, ...), custom_call_target="tpu_custom_call" | custom-call | tf_op jit(solution)/shard_map/pallas_call | solution.py:500
  78.7 0.0 copy-start
  78.7 1.1 %copy.15 = bf16[4,32,4,128]{3,2,1,0:T(4,128)(2,1)S(1)} copy(bf16[4,32,4,128]{3,1,2,0:T(8,128)(2,1)} %bitcast.35) | data formatting | bytes 262144 | tf_op jit(solution)/shard_map/transpose | solution.py:605
  79.8 1.0 %copy.16 = bf16[4,32,4,128]{3,2,1,0:T(4,128)(2,1)S(1)} copy(bf16[4,32,4,128]{3,1,2,0:T(8,128)(2,1)} %bitcast.34) | data formatting | bytes 262144 | tf_op jit(solution)/shard_map/transpose | solution.py:606
  80.8 1.7 %fusion.2 = f32[128,2048]{1,0:T(8,128)S(1)} fusion(bf16[4096,256]{1,0:T(8,128)(2,1)} %km_ref.1, s32[]{:T(128)S(6)} %select_n.4, bf16[128,512]{1,0:T(8,128)(2,1)S(1)} %bitcast.24), kind=kOutput, calls=%fused_computation.5 | convolution fusion | flops 134217728 | bytes 2162692 | tf_op jit(solution)/shard_map/dot_general | solution.py:22
  82.6 0.0 copy-done
  82.6 0.0 copy-start.1
  82.6 0.5 convolution_add_fusion.2
  83.1 0.7 copy-done.1
  83.8 0.0 copy-start.2
  83.8 0.5 convolution_add_fusion.1
  84.3 0.7 copy-done.2
  85.0 0.0 copy-start.5
  85.0 0.0 copy-start.4
  85.0 0.0 copy-start.3
  85.0 1.3 %fusion = bf16[128,2048]{1,0:T(8,128)(2,1)} fusion(f32[128,2048]{1,0:T(8,128)S(1)} %convolution_add_fusion.1, bf16[2048,256]{1,0:T(8,128)(2,1)S(1)} %copy-done.2, bf16[128,512]{1,0:T(8,128)(2,1)S(1)} %bitcast.30), kind=kOutput, calls=%fused_computation.3 | convolution fusion | flops 134742016 | bytes 2686976 | tf_op jit(solution)/shard_map/dot_general | solution.py:22
  86.3 0.0 copy-done.5
  86.3 0.7 copy.26
  87.0 0.0 copy-done.4
  87.0 0.7 copy.27
  87.7 0.0 copy-done.3
  87.7 0.7 copy.28
  (6 shorter events, 0.1 us)
Async XLA Ops:
  78.7 3.9 %copy-start = (bf16[4096,256]{1,0:T(8,128)(2,1)S(1)}, bf16[4096,256]{1,0:T(8,128)(2,1)}, u32[]{:S(2)}) copy-start(bf16[4096,256]{1,0:T(8,128)(2,1)} %vm_ref.1) | copy-start | bytes 6291460
  82.6 1.2 %copy-start.1 = (bf16[2048,256]{1,0:T(8,128)(2,1)S(1)}, bf16[2048,256]{1,0:T(8,128)(2,1)}, u32[]{:S(2)}) copy-start(bf16[2048,256]{1,0:T(8,128)(2,1)} %get-tuple-element.14) | copy-start | bytes 3145732
  83.8 1.2 %copy-start.2 = (bf16[2048,256]{1,0:T(8,128)(2,1)S(1)}, bf16[2048,256]{1,0:T(8,128)(2,1)}, u32[]{:S(2)}) copy-start(bf16[2048,256]{1,0:T(8,128)(2,1)} %get-tuple-element.15) | copy-start | bytes 3145732
  85.0 1.3 %copy-start.5 = (bf16[4,32,1024]{2,1,0:T(8,128)(2,1)S(1)}, bf16[4,32,1024]{2,1,0:T(8,128)(2,1)}, u32[]{:S(2)}) copy-start(bf16[4,32,1024]{2,1,0:T(8,128)(2,1)} %get-tuple-element.11) | copy-start | bytes 786436
  85.0 2.0 %copy-start.4 = (f32[256,256]{1,0:T(8,128)S(1)}, f32[256,256]{1,0:T(8,128)}, u32[]{:S(2)}) copy-start(f32[256,256]{1,0:T(8,128)} %get-tuple-element.24) | copy-start | bytes 786436
  85.0 2.7 %copy-start.3 = (f32[256,256]{1,0:T(8,128)S(1)}, f32[256,256]{1,0:T(8,128)}, u32[]{:S(2)}) copy-start(f32[256,256]{1,0:T(8,128)} %get-tuple-element.25) | copy-start | bytes 786436

commit v2 on v1

--- a/solution.py
+++ b/solution.py
@@ -26,14 +26,25 @@
     return index + bit - 2 * bit * ((index // bit) % 2)
 
 
+def visible(parts, keys):
+    return [
+        (a, b)
+        for a in range(parts)
+        for b in range(a + 1)
+        if (a - b - 1) * keys + 1 < WINDOW_LENGTH
+    ]
+
+
 def step_kernel(
     q_ref, g_ref, k_ref, v_ref, pos_ref, x_ref, km_ref, vm_ref,
-    dq_ref, own_ref, pair_ref, kw_ref, vw_ref, km_out, vm_out,
+    dq_out, ig_out, kw_out, vw_out,
     kv_ref, qb_ref, gb_ref, kpos_ref, s_ref, dp_ref, p_ref, ds_ref, dqb_ref, dqa_ref,
-    sum_ref, give_ref, take_ref, zs_ref, land_ref, fin_ref, all_ref, cols_ref, acc_ref,
+    sum_ref, give_ref, take_ref, land_ref, fin_ref, all_ref, cols_ref, acc_ref,
+    pair_ref, near_ref, far_ref, dq_ref, ig_ref,
     plane_send, kv_recv, kvz_send, kvp_send, kvp_recv, qg_send, qg_recv,
     x_send, x_recv, side_send, side_recv, local_sem,
-    give_send, give_recv, z_send, z_recv, col_send, ag_send, ag_recv, dq_send, dq_recv,
+    give_send, give_recv, z_send, z_recv, col_send,
+    ag_send, push_recv, relay_recv, rest_recv, dq_send, dq_recv,
 ):
     n = lax.axis_size("seq")
     cores = lax.axis_size("tp")
@@ -62,6 +73,14 @@
     power = scale * math.log2(math.e)
     other = {"seq": me, "tp": 1 - tp}
 
+    owner = home == tp
+    guest = jnp.logical_not(owner)
+
+    def sum_all(count):
+        each = count // parts
+        high = next(c for c in range(1, each + 1) if each % c == 0 and each // c <= depth)
+        return all_ref.at[:, :high, : each // high * block, :]
+
     barrier = pltpu.get_barrier_semaphore()
     for step in range(n):
         for core in range(cores):
@@ -74,8 +93,6 @@
                 )
     pl.semaphore_wait(barrier, n * cores - 1)
 
-    sent = []
-
     def when(cond, action):
         if cond is None:
             action()
@@ -90,7 +107,15 @@
             )
 
         when(cond, lambda: copy().start())
-        sent.append((cond, lambda: copy().wait_send()))
+
+    def left(src, send_sem, cond=None):
+        def wait():
+            pltpu.make_async_remote_copy(
+                src_ref=src, dst_ref=src, send_sem=send_sem, recv_sem=send_sem,
+                device_id=other, device_id_type=MESH,
+            ).wait_send()
+
+        when(cond, wait)
 
     def arrive(dst, recv_sem, cond=None):
         def wait():
@@ -136,7 +161,7 @@
                 for w, (ref, buf) in enumerate(((q_ref, qb_ref), (g_ref, gb_ref))):
                     send(
                         ref.at[:, :, cols], buf.at[:, h, rows_of(p, run), :],
-                        qg_send.at[w, i, u, h], qg_recv.at[w, p, h],
+                        qg_send.at[w], qg_recv.at[w],
                         {"seq": target, "tp": u}, jnp.logical_not(mine),
                     )
 
@@ -150,50 +175,41 @@
             column = pos_t[:, s * parts + b : s * parts + b + 1]
             kpos_ref[b, s * block : (s + 1) * block, :] = jnp.broadcast_to(column, (block, block))
 
-    def both(source):
-        place = piece(tp, source)
-        send(place, place, kvz_send.at[0, source], kv_recv.at[source],
-             {"seq": jnp.minimum(me + plane, n - 1), "tp": tp}, z + 1 < depth)
-        send(place, place, kvz_send.at[1, source], kv_recv.at[source],
-             {"seq": jnp.maximum(me - plane, 0), "tp": tp}, z > 0)
-        send(place, place, kvp_send.at[source], kvp_recv.at[source], other)
-
-    for j in range(plane):
-        index = (p + j) % plane
-        source = z * plane + index
-        if j == 0:
-            arrive(piece(tp, source), kv_recv.at[source], home != tp)
-        else:
-            arrive(piece(tp, source), kv_recv.at[source])
-        both(source)
-
-    for k in range(1, depth):
+    bits = [1 << e for e in range(depth.bit_length() - 1)]
+    order = sorted(range(depth), key=lambda k: (bin(k).count("1"), -k))
+
+    def layer(k):
+        index = z
+        for bit in bits:
+            if k & bit:
+                index = flip(index, bit)
+        return index
+
+    def lower(k):
+        return [bit for bit in reversed(bits) if k == 0 or bit < (k & -k)]
+
+    def pass_on(k):
         for j in range(plane):
-            index = (p + j) % plane
-            for way in range(2):
-                at = z - k if way == 0 else z + k
-                valid = at >= 0 if way == 0 else at < depth
-                onward = valid & (z + 1 < depth) if way == 0 else valid & (z > 0)
-                source = jnp.clip(at, 0, depth - 1) * plane + index
-                place = piece(tp, source)
-                arrive(place, kv_recv.at[source], valid)
-                to = jnp.minimum(me + plane, n - 1) if way == 0 else jnp.maximum(me - plane, 0)
-                send(place, place, kvz_send.at[way, source], kv_recv.at[source],
-                     {"seq": to, "tp": tp}, onward)
-                send(place, place, kvp_send.at[source], kvp_recv.at[source], other, valid)
-
-    for w, buf in enumerate((qb_ref, gb_ref)):
-        for j in range(plane):
-            for h in range(pair):
-                here = (p == j) & (home == tp)
-                arrive(buf.at[:, h, j * run : (j + 1) * run, :], qg_recv.at[w, j, h],
-                       jnp.logical_not(here))
-
-    for i, (src, dst) in enumerate(((km_ref, km_out), (vm_ref, vm_out))):
-        send(
-            src.at[pl.ds(pl.multiple_of((1 - tp) * features, features), features), :], dst,
-            side_send.at[i], side_recv.at[i], other,
-        )
+            source = layer(k) * plane + (p + j) % plane
+            place = piece(tp, source)
+            arrive(place, kv_recv.at[source], home != tp if k + j == 0 else None)
+            for bit in lower(k):
+                send(place, place, kvz_send, kv_recv.at[source],
+                     {"seq": flip(z, bit) * plane + p, "tp": tp})
+            send(place, place, kvp_send, kvp_recv, other)
+
+    relayed = [k for k in order if lower(k)]
+    for k in relayed:
+        pass_on(k)
+
+    def half_of(src, core):
+        return src.at[pl.ds(pl.multiple_of(core * features, features), features), :]
+
+    nearby = []
+    for i, src in enumerate((km_ref, vm_ref)):
+        send(half_of(src, 1 - tp), far_ref.at[i], side_send.at[i], side_recv.at[i], other)
+        nearby.append(pltpu.make_async_copy(half_of(src, tp), near_ref.at[i], local_sem.at[i]))
+        nearby[-1].start()
 
     def columns_of(target):
         start = ((target % half) * block_width) // x_width * x_width
@@ -201,7 +217,7 @@
 
     holder = tp == me // half
     own_columns = pltpu.make_async_copy(
-        columns_of(me), cols_ref.at[:, rows_of(me, run), :], local_sem
+        columns_of(me), cols_ref.at[:, rows_of(me, run), :], local_sem.at[2]
     )
 
     @pl.when(holder)
@@ -209,22 +225,27 @@
         own_columns.start()
 
     for slot in range(half):
-        target = tp * half + (me + slot) % half
+        target = tp * half + (me + half // 2 + slot) % half
         send(
             columns_of(target), cols_ref.at[:, rows_of(me, run), :],
-            x_send.at[slot], x_recv.at[me], {"seq": target, "tp": tp}, target != me,
+            x_send, x_recv, {"seq": target, "tp": tp}, target != me,
         )
 
-    for source in range(n):
-        arrive(kv_ref.at[1 - tp, :, source * run : (source + 1) * run, :], kvp_recv.at[source])
+    for k in order:
+        if k not in relayed:
+            pass_on(k)
+
+    fewer = (plane - 1) * run
+    for w, buf in enumerate((qb_ref, gb_ref)):
+        arrive(buf, qg_recv.at[w], guest)
+        arrive(buf.at[:, :, :fewer, :], qg_recv.at[w], owner)
+    arrive(kv_ref.at[1 - tp], kvp_recv)
+
+    tiles = visible(parts, keys)
 
     def lowest(a):
-        low = 0
-        while windowed and (a - low - 1) * keys + 1 >= WINDOW_LENGTH:
-            low += 1
-        return low
-
-    tiles = [(a, b) for a in range(parts) for b in range(lowest(a), a + 1)]
+        return min(b for c, b in tiles if c == a)
+
     where = {tile: t for t, tile in enumerate(tiles)}
 
     def sweep(body, carry):
@@ -310,7 +331,7 @@
             return carry
 
         sweep(products, 0)
-        send(give_ref.at[b], take_ref.at[b], give_send.at[b], give_recv.at[b], other)
+        send(give_ref.at[b], take_ref.at[b], give_send, give_recv.at[b], other)
         if not roomy:
             for a in uppers:
                 query_sum(a, b)
@@ -328,75 +349,94 @@
         else:
             dqa_ref[a] += acc
 
+    def exchange(b, e):
+        bit = bits[e]
+        first = depth - depth // bit
+        for t in range(depth // (2 * bit)):
+            to = flip(z, bit) % (2 * bit) + t * 2 * bit
+            rows = rows_of(to, block)
+            take_ref[b, rows, :] = sum_ref[b, rows, :].astype(jnp.bfloat16)
+            send(
+                take_ref.at[b, rows, :], land_ref.at[b, first + t], z_send,
+                z_recv.at[b, e], {"seq": flip(z, bit) * plane + p, "tp": tp},
+            )
+
     def cross(b):
         arrive(take_ref.at[b], give_recv.at[b])
-        total = sum_ref[b] + take_ref[b].astype(jnp.float32)
-        sum_ref[b] = total
-        zs_ref[b] = total.astype(jnp.bfloat16)
-        for k in range(1, depth):
-            to = (z + k) % depth
-            send(
-                zs_ref.at[b, rows_of(to, block), :], land_ref.at[b, k],
-                z_send.at[b, k], z_recv.at[b, k], {"seq": to * plane + p, "tp": tp},
-            )
+        sum_ref[b] += take_ref[b].astype(jnp.float32)
+        exchange(b, 0)
+
+    def add_landed(b, e):
+        bit = bits[e]
+        count = depth // (2 * bit)
+        first = depth - depth // bit
+        arrive(land_ref.at[b, first : first + count], z_recv.at[b, e])
+        for t in range(count):
+            rows = rows_of(z % (2 * bit) + t * 2 * bit, block)
+            sum_ref[b, rows, :] += land_ref[b, first + t].astype(jnp.float32)
+
+    def fold(e):
+        def go(b):
+            add_landed(b, e - 1)
+            exchange(b, e)
+
+        return go
 
     out_col = tp * kv_local + lane
 
     def finish(b):
-        total = sum_ref[b, rows_of(z, block), :]
-        for k in range(1, depth):
-            arrive(land_ref.at[b, k], z_recv.at[b, k])
-            total = total + land_ref[b, k].astype(jnp.float32)
-        fin_ref[b] = total.astype(jnp.bfloat16)
+        add_landed(b, len(bits) - 1)
+        fin_ref[b] = sum_ref[b, rows_of(z, block), :].astype(jnp.bfloat16)
         place = all_ref.at[b, out_col, rows_of(z, block), :]
-        slot = ag_recv.at[b, z, out_col]
-        send(fin_ref.at[b], place, col_send.at[b, 0], slot, other, home != tp)
-        for k in range(1, depth):
-            to = (z + k) % depth
-            send(fin_ref.at[b], place, col_send.at[b, k], slot, {"seq": to * plane + p, "tp": home})
-
-        @pl.when(home == tp)
+        slot = push_recv.at[b, z]
+        for bit in reversed(bits):
+            send(fin_ref.at[b], place, col_send, slot,
+                 {"seq": flip(z, bit) * plane + p, "tp": home})
+        send(fin_ref.at[b], place, col_send, slot, other, guest)
+
+        @pl.when(owner)
         def _():
             all_ref[b, out_col, rows_of(z, block), :] = fin_ref[b]
 
-    owner = home == tp
     mate_lane = kv_local - 1 - lane
     near = {"seq": z * plane + flip(p, 1), "tp": tp}
     across = {"seq": z * plane + flip(p, 2), "tp": tp}
 
     def gathered(b, at, c):
-        return all_ref.at[b, c, rows_of(at, block), :], ag_recv.at[b, at, c]
+        return all_ref.at[b, c, rows_of(at, block), :]
+
+    def later(b, k):
+        return rest_recv.at[b if k else parts]
 
     def push(b):
-        for k in range(depth):
-            at = (z + k) % depth
+        for k in order:
+            at = layer(k)
+            slot = push_recv.at[b, at]
+            arrive(all_ref.at[b, 0, : (1 if k == 0 else cores) * block, :], slot, owner)
             for role in range(cores):
-                c = role * kv_local + lane
-                place, slot = gathered(b, at, c)
-                arrive(place, slot, owner & (tp != role) if k == 0 else owner)
-                send(place, place, ag_send.at[b, at, c, 0], slot, near, owner)
-                send(place, place, ag_send.at[b, at, c, 1], slot, across, owner)
+                place = gathered(b, at, role * kv_local + lane)
+                if k:
+                    for bit in lower(k):
+                        send(place, place, ag_send.at[0], slot,
+                             {"seq": flip(z, bit) * plane + p, "tp": tp}, owner)
+                turn, rest = relay_recv.at[b, k], later(b, k)
+                send(place, place, ag_send.at[1], rest if role else turn, near, owner)
+                send(place, place, ag_send.at[2], turn if role else rest, across, owner)
 
     def relay(b):
-        for k in range(depth):
-            at = (z + k) % depth
-            c = mate_lane
-            place, slot = gathered(b, at, c)
-            arrive(place, slot, owner)
-            send(place, place, ag_send.at[b, at, c, 1], slot, across, owner)
-            c = kv_local + lane
-            place, slot = gathered(b, at, c)
-            arrive(place, slot, jnp.logical_not(owner))
-            send(place, place, ag_send.at[b, at, c, 0], slot, near, jnp.logical_not(owner))
+        for k in order:
+            at = layer(k)
+            turn, rest = relay_recv.at[b, k], later(b, k)
+            arrive(all_ref.at[b, 0, :block, :], turn)
+            place = gathered(b, at, mate_lane)
+            send(place, place, ag_send.at[3], rest, across, owner)
+            place = gathered(b, at, kv_local + lane)
+            send(place, place, ag_send.at[3], rest, near, guest)
 
     def collect(b):
-        for k in range(depth):
-            at = (z + k) % depth
-            place, slot = gathered(b, at, kv_local + mate_lane)
-            arrive(place, slot)
-            for c in (lane, mate_lane):
-                place, slot = gathered(b, at, c)
-                arrive(place, slot, jnp.logical_not(owner))
+        count = (depth - 1) * block
+        arrive(all_ref.at[b, 0, :count, :], rest_recv.at[b], owner)
+        arrive(all_ref.at[b, :3, :count, :], rest_recv.at[b], guest)
 
     def weigh(b, first):
         grads = [all_ref[b, c] for c in range(cores * kv_local)]
@@ -411,9 +451,7 @@
         def _():
             own_columns.wait()
 
-        for step in range(1, n):
-            source = (me + step) % n
-            arrive(cols_ref.at[:, rows_of(source, run), :], x_recv.at[source], holder)
+        arrive(cols_ref.at[:, : (n - 1) * run, :], x_recv, holder)
         send(cols_ref, cols_ref, side_send.at[2], side_recv.at[2], other, holder)
         arrive(cols_ref, side_recv.at[2], jnp.logical_not(holder))
 
@@ -430,7 +468,7 @@
                 mine = (p == j) & (home == tp)
                 src = dqb_ref.at[:, h, j * run : (j + 1) * run, :]
                 send(
-                    src, dq_ref.at[:, :, cols], dq_send.at[h, j], dq_recv.at[lane, tp, h],
+                    src, dq_ref.at[:, :, cols], dq_send, dq_recv,
                     {"seq": z * plane + j, "tp": home}, jnp.logical_not(mine),
                 )
 
@@ -438,42 +476,122 @@
                 def _():
                     dq_ref[:, :, cols] = dqb_ref[:, h, j * run : (j + 1) * run, :]
 
+    own_rows = rows_of(me, run)
+    leaving = []
+
+    def put(src, dst):
+        leaving.append(pltpu.make_async_copy(src, dst, local_sem.at[3 + len(leaving)]))
+        leaving[-1].start()
+
+    def answers():
+        arrive(dqb_ref, dq_recv, guest)
+        arrive(dqb_ref.at[:, :, :fewer, :], dq_recv, owner)
+        put(dq_ref, dq_out)
+
+    def swap():
+        arrive(all_ref.at[:, 0, :block, :], rest_recv.at[parts], owner)
+        arrive(all_ref.at[:, :3, :block, :], rest_recv.at[parts], guest)
+        send(all_ref.at[:, :, own_rows, :], pair_ref, side_send.at[3], side_recv.at[3], other)
+
+    def inputs():
+        for copy in nearby:
+            copy.wait()
+        for i in range(2):
+            arrive(far_ref.at[i], side_recv.at[i])
+        arrive(pair_ref, side_recv.at[3])
+        rows = parts * run
+        grads = [all_ref[:, c, own_rows, :].reshape(rows, HEAD_SIZE) for c in range(2 * kv_local)]
+        grads += [pair_ref[:, c].reshape(rows, HEAD_SIZE) for c in range(2 * kv_local)]
+        grads = jnp.concatenate(grads, axis=1)
+        for f in range(0, features, CHUNK):
+            tile = slice(f, min(f + CHUNK, features))
+            weights = [ref[i, tile, :] for ref in (near_ref, far_ref) for i in range(2)]
+            out = dot(grads, jnp.concatenate(weights, axis=1), NT)
+            ig_ref[:, tile] = out.astype(jnp.bfloat16)
+        put(ig_ref, ig_out)
+
+    stages = [backward, cross] + [fold(e) for e in range(1, len(bits))] + [finish, push]
     last = parts - 1
-    for tick in range(parts + 2):
-        for level, stage in enumerate((backward, cross, finish)):
+    for tick in range(last + len(stages)):
+        for level, stage in enumerate(stages):
             b = last - (tick - level)
             if 0 <= b <= last:
                 stage(b)
-        if tick >= 2:
-            push(last - (tick - 2))
-        if tick == parts - 1:
+        if tick == last:
             queries()
     for b in reversed(range(parts)):
         relay(b)
+    swap()
     columns()
+    answers()
     for b in reversed(range(parts)):
+        if b == 0:
+            inputs()
         collect(b)
         weigh(b, b == last)
 
-    own_rows = rows_of(me, run)
-    send(all_ref.at[:, :, own_rows, :], pair_ref, side_send.at[3], side_recv.at[3], other)
-    own_ref[...] = all_ref[:, :, own_rows, :]
     middle = kv_local * HEAD_SIZE
-    kw_ref[...] = acc_ref[:, :middle]
-    vw_ref[...] = acc_ref[:, middle:]
+    put(acc_ref.at[:, :middle], kw_out)
+    put(acc_ref.at[:, middle:], vw_out)
+    for copy in leaving:
+        copy.wait()
 
     for i in range(kv_local):
-        for u in range(cores):
-            for h in range(pair):
-                first = (i * GROUP + u * pair + h) * HEAD_SIZE
-                here = (p == tp * kv_local + i) & (tp == u)
-                arrive(dq_ref.at[:, :, first : first + HEAD_SIZE], dq_recv.at[i, u, h],
-                       jnp.logical_not(here))
-    for i, dst in enumerate((km_out, vm_out)):
-        arrive(dst, side_recv.at[i])
-    arrive(pair_ref, side_recv.at[3])
-    for cond, wait in sent:
-        when(cond, wait)
+        for role in range(cores):
+            mine = (tp * kv_local + i == p) & (tp == role)
+            left(piece(role, me), plane_send.at[i, role], jnp.logical_not(mine))
+    for w, buf in ((0, qb_ref), (1, gb_ref)):
+        left(buf, qg_send.at[w], guest)
+        left(buf.at[:, :, :fewer, :], qg_send.at[w], owner)
+    moves = sum(len(lower(k)) for k in order)
+    left(kv_ref.at[0, :, : moves * block, :], kvz_send)
+    left(kv_ref.at[0], kvp_send)
+    left(cols_ref.at[:, : half * run, :], x_send, jnp.logical_not(holder))
+    left(cols_ref.at[:, : (half - 1) * run, :], x_send, holder)
+    left(cols_ref, side_send.at[2], holder)
+    for i in range(2):
+        left(far_ref.at[i], side_send.at[i])
+    left(pair_ref, side_send.at[3])
+    left(give_ref, give_send)
+    left(take_ref.at[:, : (depth - 1) * block, :], z_send)
+    left(dqb_ref, dq_send, guest)
+    left(dqb_ref.at[:, :, :fewer, :], dq_send, owner)
+    ways = len(bits)
+    left(sum_all(ways * parts), col_send, owner)
+    left(sum_all((ways + 1) * parts), col_send, guest)
+    left(sum_all((moves - ways) * cores * parts), ag_send.at[0], owner)
+    left(sum_all(depth * cores * parts), ag_send.at[1], owner)
+    left(sum_all(depth * cores * parts), ag_send.at[2], owner)
+    left(sum_all(depth * parts), ag_send.at[3])
+
+
+def deliver_kernel(*refs):
+    count = (len(refs) - 1) // 3
+    ins, outs, held = refs[:count], refs[count : 2 * count], refs[2 * count : 3 * count]
+    sems = refs[3 * count]
+    moves = []
+    for i in range(count):
+        moves.append(pltpu.make_async_copy(ins[i], held[i], sems.at[0, i]))
+        moves[-1].start()
+    for i in range(count):
+        moves[i].wait()
+        moves.append(pltpu.make_async_copy(held[i], outs[i], sems.at[1, i]))
+        moves[-1].start()
+    for move in moves[count:]:
+        move.wait()
+
+
+def deliver(*arrays):
+    hbm = pl.BlockSpec(memory_space=pl.ANY)
+    count = len(arrays)
+    return pl.pallas_call(
+        deliver_kernel,
+        out_shape=tuple(jax.ShapeDtypeStruct(a.shape, a.dtype) for a in arrays),
+        in_specs=[hbm] * count,
+        out_specs=(hbm,) * count,
+        scratch_shapes=[pltpu.VMEM(a.shape, a.dtype) for a in arrays]
+        + [pltpu.SemaphoreType.DMA((2, count))],
+    )(*arrays)
 
 
 def step(n, q, g, k, v, pos, x, km, vm):
@@ -486,12 +604,13 @@
     plane = cores * kv_local
     pair = GROUP // cores
     depth = n // plane
+    levels = depth.bit_length() - 1
     block = plane * run
     keys = n * run
     wide = pair * block
     x_width = max(cores * features // n, 128)
     roomy = parts * keys <= 4096
-    tiles = parts * (parts + 1) // 2
+    tiles = len(visible(parts, keys))
     vmem = pl.BlockSpec(memory_space=pltpu.VMEM)
     hbm = pl.BlockSpec(memory_space=pl.ANY)
     kind = jnp.bfloat16
@@ -501,15 +620,12 @@
         step_kernel,
         out_shape=(
             jax.ShapeDtypeStruct((parts, run, width), kind),
-            jax.ShapeDtypeStruct((parts, 2 * kv_local, run, HEAD_SIZE), kind),
-            jax.ShapeDtypeStruct((parts, 2 * kv_local, run, HEAD_SIZE), kind),
+            jax.ShapeDtypeStruct((parts * run, features), kind),
             jax.ShapeDtypeStruct((x_width, kv_width), real),
             jax.ShapeDtypeStruct((x_width, kv_width), real),
-            jax.ShapeDtypeStruct((features, kv_width), kind),
-            jax.ShapeDtypeStruct((features, kv_width), kind),
         ),
         in_specs=[vmem] * 5 + [hbm] * 3,
-        out_specs=(vmem, vmem, vmem, vmem, vmem, hbm, hbm),
+        out_specs=(hbm,) * 4,
         scratch_shapes=[
             pltpu.VMEM((2, parts, keys, HEAD_SIZE), kind),
             pltpu.VMEM((parts, pair, block, HEAD_SIZE), kind),
@@ -524,33 +640,39 @@
             pltpu.VMEM((parts, keys, HEAD_SIZE), real),
             pltpu.VMEM((parts, keys, HEAD_SIZE), kind),
             pltpu.VMEM((parts, keys, HEAD_SIZE), kind),
-            pltpu.VMEM((parts, keys, HEAD_SIZE), kind),
-            pltpu.VMEM((parts, depth, block, HEAD_SIZE), kind),
+            pltpu.VMEM((parts, depth - 1, block, HEAD_SIZE), kind),
             pltpu.VMEM((parts, block, HEAD_SIZE), kind),
             pltpu.VMEM((parts, 2 * kv_local, keys, HEAD_SIZE), kind),
             pltpu.VMEM((parts, keys, x_width), kind),
             pltpu.VMEM((x_width, 2 * kv_width), real),
+            pltpu.VMEM((parts, 2 * kv_local, run, HEAD_SIZE), kind),
+            pltpu.VMEM((2, features, kv_width), kind),
+            pltpu.VMEM((2, features, kv_width), kind),
+            pltpu.VMEM((parts, run, width), kind),
+            pltpu.VMEM((parts * run, features), kind),
             dma((kv_local, cores)),
             dma((n,)),
-            dma((2, n)),
-            dma((n,)),
-            dma((n,)),
-            dma((2, kv_local, cores, pair)),
-            dma((2, plane, pair)),
-            dma((n // cores,)),
-            dma((n,)),
+            dma,
+            dma,
+            dma,
+            dma((2,)),
+            dma((2,)),
+            dma,
+            dma,
             dma((4,)),
             dma((4,)),
+            dma((7,)),
             dma,
             dma((parts,)),
-            dma((parts,)),
+            dma,
+            dma((parts, levels)),
+            dma,
+            dma((4,)),
             dma((parts, depth)),
             dma((parts, depth)),
-            dma((parts, depth)),
-            dma((parts, depth, cores * kv_local, 2)),
-            dma((parts, depth, cores * kv_local)),
-            dma((pair, plane)),
-            dma((kv_local, cores, pair)),
+            dma((parts + 1,)),
+            dma,
+            dma,
         ],
         compiler_params=pltpu.CompilerParams(
             vmem_limit_bytes=63 * 2**20, collective_id=0, has_side_effects=True
@@ -581,7 +703,6 @@
     run_placement,
 ):
     seq_index = lax.axis_index("seq")
-    tp_index = lax.axis_index("tp")
     seq_count = run_placement.shape[0]
     rows_here = query_rows.shape[0]
     kv_width = key_rows.shape[1]
@@ -591,7 +712,7 @@
     def cut(array):
         return array.reshape(parts, rows_here // parts, array.shape[1])
 
-    query_grad, kv_grad, kv_mate, key_weight, value_weight, key_far, value_far = step(
+    query_grad, input_grad, key_weight, value_weight = step(
         seq_count,
         cut(query_rows),
         cut(output_grad),
@@ -602,16 +723,9 @@
         key_matrix,
         value_matrix,
     )
-    kv_grad = jnp.swapaxes(kv_grad, 1, 2).reshape(rows_here, 2 * kv_width)
-    kv_mate = jnp.swapaxes(kv_mate, 1, 2).reshape(rows_here, 2 * kv_width)
-    key_near = lax.dynamic_slice_in_dim(key_matrix, tp_index * features, features, 0)
-    value_near = lax.dynamic_slice_in_dim(value_matrix, tp_index * features, features, 0)
-    input_grad = (
-        dot(kv_grad[:, :kv_width], key_near, NT)
-        + dot(kv_grad[:, kv_width:], value_near, NT)
-        + dot(kv_mate[:, :kv_width], key_far, NT)
-        + dot(kv_mate[:, kv_width:], value_far, NT)
-    ).astype(jnp.bfloat16)
+    query_grad, input_grad, key_weight, value_weight = deliver(
+        query_grad, input_grad, key_weight, value_weight
+    )
     block_width = 2 * features // seq_count
     if key_weight.shape[0] != block_width:
         shift = (seq_index * block_width) % key_weight.shape[0]

time: 89.7 us -> 74 us (0.82)
  the two profiles are of different devices: /device:TPU:0 before, /device:TPU:7 now
where the time goes in v2:
time: 74 us; the launch traced here: 73.8 us
  Pallas kernels  71.3 us (96%)
  local copies, waits for them, and re-layouts  1.04 us (1%)
  other arithmetic  0.78 us (1%)
    pallas_call x1, Pallas kernels, step(): pl.pallas_call(step_kernel, out_shape=(jax.ShapeDtypeStruct((parts, run,...  69.1 us
    pallas_call x1, Pallas kernels, deliver(): pl.pallas_call(deliver_kernel, out_shape=tuple((jax.ShapeDtypeStruct(a.sh...  2.16 us

profile of v2, /device:TPU:7, one launch (start us, length us, event | category | flops | bytes accessed | tf_op | source)
XLA Modules:
  0.0 73.8 jit_solution(17452784392777282141)
XLA Ops:
  0.7 0.1 add.33
  0.7 0.8 %add_bitcast_fusion = s32[16,16]{0,1:T(8,128)S(1)} fusion(s32[16,16]{1,0:T(8,128)} %param.15, s32[16]{0:T(128)S(1)} %iota_multiply_fusion), kind=kLoop, calls=%fused_computation.1 | loop fusion | flops 512 | bytes 2112 | tf_op jit(solution)/shard_map/transpose | solution.py:687
  1.5 0.1 copy.13
  1.6 0.1 add.30
  1.7 0.1 add.31
  1.8 0.7 convert_element_type.9.pos_ref
  2.5 69.1 %shard_map.111 = (bf16[4,32,1024]{2,1,0:T(8,128)(2,1)}, bf16[128,2048]{1,0:T(8,128)(2,1)}, f32[256,256]{1,0:T(8,128)}, f32[256,256]{1,0:T(8,128)}) custom-call(bf16[4,32,1024]{2,1,0:T(8,128)(2,1)} %bitcast.11, bf16[4,32,1024]{2,1,0:T(8,128)(2,1)} %bitcast.12, bf16[4,32,256]{2,1,0:T(8,128)(2,1)} %bitcast.13, bf16[4,32,256]{2,1,0:T(8,128)(2,1)} %bitcast.14, ...), custom_call_target="tpu_custom_call" | custom-call | tf_op jit(solution)/shard_map/pallas_call | solution.py:619
  71.6 2.2 %shard_map.112 = (bf16[4,32,1024]{2,1,0:T(8,128)(2,1)}, bf16[128,2048]{1,0:T(8,128)(2,1)}, f32[256,256]{1,0:T(8,128)}, f32[256,256]{1,0:T(8,128)}) custom-call(bf16[4,32,1024]{2,1,0:T(8,128)(2,1)} %get-tuple-element.12.refs_0_, bf16[128,2048]{1,0:T(8,128)(2,1)} %get-tuple-element.13.refs_1_, f32[256,256]{1,0:T(8,128)} %get-tuple-element.14.refs_2_, ...), custom_call_target="tpu_custom_call" | custom-call | tf_op jit(solution)/shard_map/pallas_call | solution.py:587
  (4 shorter events, 0.0 us)

commit v3 on v2

--- a/solution.py
+++ b/solution.py
@@ -36,15 +36,16 @@
 
 
 def step_kernel(
-    q_ref, g_ref, k_ref, v_ref, pos_ref, x_ref, km_ref, vm_ref,
-    dq_out, ig_out, kw_out, vw_out,
+    q_in, g_in, k_in, v_in, place_ref, x_ref, km_ref, vm_ref,
+    dq_ref, ig_ref, kw_ref, vw_ref,
     kv_ref, qb_ref, gb_ref, kpos_ref, s_ref, dp_ref, p_ref, ds_ref, dqb_ref, dqa_ref,
-    sum_ref, give_ref, take_ref, land_ref, fin_ref, all_ref, cols_ref, acc_ref,
-    pair_ref, near_ref, far_ref, dq_ref, ig_ref,
+    sum_ref, give_ref, take_ref, land_ref, wk_ref, xs_ref, acc_ref,
+    own_ref, out_ref, got_ref, near_ref, far_ref, q_ref, g_ref, k_ref, v_ref, pos_ref,
     plane_send, kv_recv, kvz_send, kvp_send, kvp_recv, qg_send, qg_recv,
-    x_send, x_recv, side_send, side_recv, local_sem,
-    give_send, give_recv, z_send, z_recv, col_send,
-    ag_send, push_recv, relay_recv, rest_recv, dq_send, dq_recv,
+    x_sent, x_recv, side_send, side_recv, local_sem,
+    give_send, give_recv, z_send, z_recv,
+    xp_send, xr_recv, xd_send, xd_recv, wk_send, wk_recv, own_sem, share_sem,
+    dq_send, dq_recv,
 ):
     n = lax.axis_size("seq")
     cores = lax.axis_size("tp")
@@ -66,9 +67,7 @@
     roomy = dp_ref.shape[0] > 1
     windowed = parts * keys > WINDOW_LENGTH
     features = x_ref.shape[2]
-    half = n // cores
-    x_width = cols_ref.shape[2]
-    block_width = features // half
+    x_width = xs_ref.shape[2]
     scale = 1.0 / math.sqrt(HEAD_SIZE)
     power = scale * math.log2(math.e)
     other = {"seq": me, "tp": 1 - tp}
@@ -76,10 +75,107 @@
     owner = home == tp
     guest = jnp.logical_not(owner)
 
-    def sum_all(count):
-        each = count // parts
-        high = next(c for c in range(1, each + 1) if each % c == 0 and each // c <= depth)
-        return all_ref.at[:, :high, : each // high * block, :]
+    def when(cond, action):
+        if cond is None:
+            action()
+        else:
+            pl.when(cond)(action)
+
+    def send(src, dst, send_sem, recv_sem, device, cond=None):
+        def copy():
+            return pltpu.make_async_remote_copy(
+                src_ref=src, dst_ref=dst, send_sem=send_sem, recv_sem=recv_sem,
+                device_id=device, device_id_type=MESH,
+            )
+
+        when(cond, lambda: copy().start())
+
+    def left(src, send_sem, cond=None):
+        def wait():
+            pltpu.make_async_remote_copy(
+                src_ref=src, dst_ref=src, send_sem=send_sem, recv_sem=send_sem,
+                device_id=other, device_id_type=MESH,
+            ).wait_send()
+
+        when(cond, wait)
+
+    def arrive(dst, recv_sem, cond=None):
+        def wait():
+            pltpu.make_async_remote_copy(
+                src_ref=dst, dst_ref=dst, send_sem=recv_sem, recv_sem=recv_sem,
+                device_id=other, device_id_type=MESH,
+            ).wait_recv()
+
+        when(cond, wait)
+
+    def rows_of(index, count):
+        return pl.ds(pl.multiple_of(index * count, count), count)
+
+    def lanes_of(index):
+        return pl.ds(pl.multiple_of(index * HEAD_SIZE, HEAD_SIZE), HEAD_SIZE)
+
+    bits = [1 << e for e in range(depth.bit_length() - 1)]
+    order = sorted(range(depth), key=lambda k: (bin(k).count("1"), -k))
+
+    def layer(k):
+        index = z
+        for bit in bits:
+            if k & bit:
+                index = flip(index, bit)
+        return index
+
+    def lower(k):
+        return [bit for bit in reversed(bits) if k == 0 or bit < (k & -k)]
+
+    layers = depth // cores
+    holder = tp == z // layers
+    flips = ((1,), (2,), (1, 2))
+
+    def block_of(source):
+        return xs_ref.at[:, rows_of(source, run), :]
+
+    def columns_of(target):
+        start = (target % layers) * x_width
+        return x_ref.at[:, :, pl.ds(pl.multiple_of(start, x_width), x_width)]
+
+    staged = []
+    for src, dst in ((k_in, k_ref), (v_in, v_ref), (q_in, q_ref), (g_in, g_ref)):
+        staged.append(pltpu.make_async_copy(src, dst, local_sem.at[3 + len(staged)]))
+        staged[-1].start()
+
+    own_columns = pltpu.make_async_copy(columns_of(z), block_of(me), local_sem.at[2])
+    pl.when(holder)(own_columns.start)
+
+    def x_send(slot, early):
+        target = tp * layers + (z + layers - 1 - slot) % layers
+        clear = (target > z) == (z % 2 == 1)
+        now = clear if early else jnp.logical_not(clear)
+        send(
+            columns_of(target), block_of(me), x_sent, x_recv.at[z],
+            {"seq": target * plane + p, "tp": tp}, (target != z) & now,
+        )
+
+    def turned(index, ways):
+        for bit in ways:
+            index = flip(index, bit)
+        return index
+
+    def x_push(k):
+        block = block_of(layer(k) * plane + p)
+        if k == 0:
+            pl.when(holder)(own_columns.wait)
+        else:
+            arrive(block, x_recv.at[layer(k)], holder)
+        for way, ways in enumerate(flips):
+            send(block, block, xp_send, xr_recv.at[way, k],
+                 {"seq": z * plane + turned(p, ways), "tp": tp}, holder)
+        send(block, block, xd_send, xd_recv, other, holder)
+
+    def x_relay(k):
+        for way, ways in enumerate(flips):
+            block = block_of(layer(k) * plane + turned(p, ways))
+            arrive(block, xr_recv.at[way, k], holder)
+            send(block, block, xd_send, xd_recv, other, holder)
 
     barrier = pltpu.get_barrier_semaphore()
     for step in range(n):
@@ -93,44 +189,8 @@
                 )
     pl.semaphore_wait(barrier, n * cores - 1)
 
-    def when(cond, action):
-        if cond is None:
-            action()
-        else:
-            pl.when(cond)(action)
-
-    def send(src, dst, send_sem, recv_sem, device, cond=None):
-        def copy():
-            return pltpu.make_async_remote_copy(
-                src_ref=src, dst_ref=dst, send_sem=send_sem, recv_sem=recv_sem,
-                device_id=device, device_id_type=MESH,
-            )
-
-        when(cond, lambda: copy().start())
-
-    def left(src, send_sem, cond=None):
-        def wait():
-            pltpu.make_async_remote_copy(
-                src_ref=src, dst_ref=src, send_sem=send_sem, recv_sem=send_sem,
-                device_id=other, device_id_type=MESH,
-            ).wait_send()
-
-        when(cond, wait)
-
-    def arrive(dst, recv_sem, cond=None):
-        def wait():
-            pltpu.make_async_remote_copy(
-                src_ref=dst, dst_ref=dst, send_sem=recv_sem, recv_sem=recv_sem,
-                device_id=other, device_id_type=MESH,
-            ).wait_recv()
-
-        when(cond, wait)
-
-    def rows_of(index, count):
-        return pl.ds(pl.multiple_of(index * count, count), count)
-
-    def lanes_of(index):
-        return pl.ds(pl.multiple_of(index * HEAD_SIZE, HEAD_SIZE), HEAD_SIZE)
+    for copy in staged:
+        copy.wait()
 
     def piece(role, source):
         return kv_ref.at[role, :, rows_of(source, run), :]
@@ -169,24 +229,28 @@
                     def _():
                         buf[:, h, rows_of(p, run), :] = ref[:, :, cols]
 
+    x_push(0)
+
+    short = parts * run // n
+    count = run // short
+    column = lax.broadcasted_iota(jnp.int32, (n, block), 1)
+    row = lax.broadcasted_iota(jnp.int32, (n, block), 0)
+    slot = column % run // short
+    table = place_ref[...].astype(jnp.bfloat16)
+    for s in range(depth):
+        picks = (row == s * plane + column // run).astype(jnp.bfloat16)
+        slots = dot(table, picks, NN)
+        for a in range(parts):
+            chosen = jnp.where(row == a * count + slot, slots, 0.0)
+            start = (a * count + slot[:1]) * (parts * run) + column[:1] % short
+            pos_ref[s * parts + a : s * parts + a + 1, :] = (
+                jnp.sum(chosen, axis=0, keepdims=True) * short + start.astype(jnp.float32)
+            )
     pos_t = jnp.transpose(pos_ref[...])
     for b in range(parts):
         for s in range(depth):
             column = pos_t[:, s * parts + b : s * parts + b + 1]
             kpos_ref[b, s * block : (s + 1) * block, :] = jnp.broadcast_to(column, (block, block))
-
-    bits = [1 << e for e in range(depth.bit_length() - 1)]
-    order = sorted(range(depth), key=lambda k: (bin(k).count("1"), -k))
-
-    def layer(k):
-        index = z
-        for bit in bits:
-            if k & bit:
-                index = flip(index, bit)
-        return index
-
-    def lower(k):
-        return [bit for bit in reversed(bits) if k == 0 or bit < (k & -k)]
 
     def pass_on(k):
         for j in range(plane):
@@ -199,7 +263,10 @@
             send(place, place, kvp_send, kvp_recv, other)
 
     relayed = [k for k in order if lower(k)]
-    for k in relayed:
+    pass_on(0)
+    for slot in range(layers):
+        x_send(slot, True)
+    for k in relayed[1:]:
         pass_on(k)
 
     def half_of(src, core):
@@ -211,25 +278,8 @@
         nearby.append(pltpu.make_async_copy(half_of(src, tp), near_ref.at[i], local_sem.at[i]))
         nearby[-1].start()
 
-    def columns_of(target):
-        start = ((target % half) * block_width) // x_width * x_width
-        return x_ref.at[:, :, pl.ds(pl.multiple_of(start, x_width), x_width)]
-
-    holder = tp == me // half
-    own_columns = pltpu.make_async_copy(
-        columns_of(me), cols_ref.at[:, rows_of(me, run), :], local_sem.at[2]
-    )
-
-    @pl.when(holder)
-    def _():
-        own_columns.start()
-
-    for slot in range(half):
-        target = tp * half + (me + half // 2 + slot) % half
-        send(
-            columns_of(target), cols_ref.at[:, rows_of(me, run), :],
-            x_send, x_recv, {"seq": target, "tp": tp}, target != me,
-        )
+    for slot in range(layers):
+        x_send(slot, False)
 
     for k in order:
         if k not in relayed:
@@ -253,6 +303,7 @@
             return body(slice(0, keys), carry)
         return lax.fori_loop(0, keys // sub, lambda i, c: body(rows_of(i, sub), c), carry)
 
+    x_relay(0)
     inverse, delta = [], []
     for a in range(parts):
         qa = qb_ref[a].reshape(wide, HEAD_SIZE)
@@ -382,78 +433,64 @@
 
         return go
 
-    out_col = tp * kv_local + lane
-
     def finish(b):
         add_landed(b, len(bits) - 1)
-        fin_ref[b] = sum_ref[b, rows_of(z, block), :].astype(jnp.bfloat16)
-        place = all_ref.at[b, out_col, rows_of(z, block), :]
-        slot = push_recv.at[b, z]
-        for bit in reversed(bits):
-            send(fin_ref.at[b], place, col_send, slot,
-                 {"seq": flip(z, bit) * plane + p, "tp": home})
-        send(fin_ref.at[b], place, col_send, slot, other, guest)
-
-        @pl.when(owner)
-        def _():
-            all_ref[b, out_col, rows_of(z, block), :] = fin_ref[b]
-
-    mate_lane = kv_local - 1 - lane
-    near = {"seq": z * plane + flip(p, 1), "tp": tp}
-    across = {"seq": z * plane + flip(p, 2), "tp": tp}
-
-    def gathered(b, at, c):
-        return all_ref.at[b, c, rows_of(at, block), :]
-
-    def later(b, k):
-        return rest_recv.at[b if k else parts]
-
-    def push(b):
+        rows = rows_of(z, block)
+        wk_ref[b, rows, :] = sum_ref[b, rows, :].astype(jnp.bfloat16)
+        carry(b, 0)
+
+    def carry(b, k):
+        place = wk_ref.at[b, rows_of(layer(k), block), :]
+        for bit in lower(k):
+            send(place, place, wk_send, wk_recv.at[b, layer(k)],
+                 {"seq": flip(z, bit) * plane + p, "tp": tp})
+
+    def collect(b, k):
+        arrive(wk_ref.at[b, rows_of(layer(k), block), :], wk_recv.at[b, layer(k)])
+
+    def hand(b):
+        for k in relayed[1:]:
+            collect(b, k)
+            carry(b, k)
+
+    def gather(b):
         for k in order:
-            at = layer(k)
-            slot = push_recv.at[b, at]
-            arrive(all_ref.at[b, 0, : (1 if k == 0 else cores) * block, :], slot, owner)
-            for role in range(cores):
-                place = gathered(b, at, role * kv_local + lane)
-                if k:
-                    for bit in lower(k):
-                        send(place, place, ag_send.at[0], slot,
-                             {"seq": flip(z, bit) * plane + p, "tp": tp}, owner)
-                turn, rest = relay_recv.at[b, k], later(b, k)
-                send(place, place, ag_send.at[1], rest if role else turn, near, owner)
-                send(place, place, ag_send.at[2], turn if role else rest, across, owner)
-
-    def relay(b):
-        for k in order:
-            at = layer(k)
-            turn, rest = relay_recv.at[b, k], later(b, k)
-            arrive(all_ref.at[b, 0, :block, :], turn)
-            place = gathered(b, at, mate_lane)
-            send(place, place, ag_send.at[3], rest, across, owner)
-            place = gathered(b, at, kv_local + lane)
-            send(place, place, ag_send.at[3], rest, near, guest)
-
-    def collect(b):
-        count = (depth - 1) * block
-        arrive(all_ref.at[b, 0, :count, :], rest_recv.at[b], owner)
-        arrive(all_ref.at[b, :3, :count, :], rest_recv.at[b], guest)
+            if k not in relayed:
+                collect(b, k)
 
     def weigh(b, first):
-        grads = [all_ref[b, c] for c in range(cores * kv_local)]
-        part = dot(cols_ref[b], jnp.concatenate(grads, axis=1), TN)
+        part = dot(wk_ref[b], xs_ref[b], TN)
         if first:
             acc_ref[...] = part
         else:
             acc_ref[...] += part
 
-    def columns():
-        @pl.when(holder)
+    def own_send():
+        for j in range(plane):
+            src = wk_ref.at[:, rows_of(z * plane + j, run), :]
+            for core in range(cores):
+                mine = (p == j) & (tp == core)
+                index = tp * plane + p
+                send(src, own_ref.at[index], own_sem.at[0], own_sem.at[1],
+                     {"seq": z * plane + j, "tp": core}, jnp.logical_not(mine))
+
+                @pl.when(mine)
+                def _():
+                    own_ref[index] = wk_ref[:, rows_of(z * plane + j, run), :]
+
+    def share():
+        grads = jnp.transpose(acc_ref[...]).astype(jnp.bfloat16)
+        rows = grads.shape[0] // plane
+        for j in range(plane):
+            out_ref[j] = grads[j * rows : (j + 1) * rows]
+        for ways in ((1, 2), (1,), (2,), ()):
+            j = turned(p, ways)
+            send(out_ref.at[j], got_ref.at[tp * kv_local + lane], share_sem.at[0], share_sem.at[1],
+                 {"seq": z * plane + j, "tp": home}, None if ways else guest)
+
+        @pl.when(owner)
         def _():
-            own_columns.wait()
-
-        arrive(cols_ref.at[:, : (n - 1) * run, :], x_recv, holder)
-        send(cols_ref, cols_ref, side_send.at[2], side_recv.at[2], other, holder)
-        arrive(cols_ref, side_recv.at[2], jnp.logical_not(holder))
+            got_ref[tp * kv_local + lane] = out_ref[p]
 
     def queries():
         for a in range(parts):
@@ -476,66 +513,67 @@
                 def _():
                     dq_ref[:, :, cols] = dqb_ref[:, h, j * run : (j + 1) * run, :]
 
-    own_rows = rows_of(me, run)
-    leaving = []
-
-    def put(src, dst):
-        leaving.append(pltpu.make_async_copy(src, dst, local_sem.at[3 + len(leaving)]))
-        leaving[-1].start()
-
     def answers():
         arrive(dqb_ref, dq_recv, guest)
         arrive(dqb_ref.at[:, :, :fewer, :], dq_recv, owner)
-        put(dq_ref, dq_out)
-
-    def swap():
-        arrive(all_ref.at[:, 0, :block, :], rest_recv.at[parts], owner)
-        arrive(all_ref.at[:, :3, :block, :], rest_recv.at[parts], guest)
-        send(all_ref.at[:, :, own_rows, :], pair_ref, side_send.at[3], side_recv.at[3], other)
 
     def inputs():
         for copy in nearby:
             copy.wait()
         for i in range(2):
             arrive(far_ref.at[i], side_recv.at[i])
-        arrive(pair_ref, side_recv.at[3])
+        arrive(own_ref.at[: cores * plane - 1], own_sem.at[1])
         rows = parts * run
-        grads = [all_ref[:, c, own_rows, :].reshape(rows, HEAD_SIZE) for c in range(2 * kv_local)]
-        grads += [pair_ref[:, c].reshape(rows, HEAD_SIZE) for c in range(2 * kv_local)]
+        grads = [
+            own_ref[role * plane + core * kv_local + i].reshape(rows, HEAD_SIZE)
+            for core in (tp, 1 - tp)
+            for role in range(2)
+            for i in range(kv_local)
+        ]
         grads = jnp.concatenate(grads, axis=1)
         for f in range(0, features, CHUNK):
             tile = slice(f, min(f + CHUNK, features))
             weights = [ref[i, tile, :] for ref in (near_ref, far_ref) for i in range(2)]
             out = dot(grads, jnp.concatenate(weights, axis=1), NT)
             ig_ref[:, tile] = out.astype(jnp.bfloat16)
-        put(ig_ref, ig_out)
-
-    stages = [backward, cross] + [fold(e) for e in range(1, len(bits))] + [finish, push]
+
     last = parts - 1
+    for b in reversed(range(parts)):
+        backward(b)
+        if b < last:
+            cross(b + 1)
+        if b == last - 1:
+            x_push(1)
+    cross(0)
+    for k in range(2, depth):
+        x_push(k)
+    stages = [fold(e) for e in range(1, len(bits))] + [finish, hand]
     for tick in range(last + len(stages)):
         for level, stage in enumerate(stages):
             b = last - (tick - level)
             if 0 <= b <= last:
                 stage(b)
         if tick == last:
+            x_relay(1)
             queries()
+        if tick == last + 1:
+            x_relay(2)
+    for k in range(3, depth):
+        x_relay(k)
+    own_send()
+    arrive(xs_ref, xd_recv, jnp.logical_not(holder))
     for b in reversed(range(parts)):
-        relay(b)
-    swap()
-    columns()
+        gather(b)
+        weigh(b, b == last)
+    share()
     answers()
-    for b in reversed(range(parts)):
-        if b == 0:
-            inputs()
-        collect(b)
-        weigh(b, b == last)
-
-    middle = kv_local * HEAD_SIZE
-    put(acc_ref.at[:, :middle], kw_out)
-    put(acc_ref.at[:, middle:], vw_out)
-    for copy in leaving:
-        copy.wait()
-
+    inputs()
+    arrive(got_ref, share_sem.at[1], guest)
+    arrive(got_ref.at[: cores * kv_local - 1], share_sem.at[1], owner)
+    for role, held in enumerate((kw_ref, vw_ref)):
+        for i in range(kv_local):
+            cols = slice(i * HEAD_SIZE, (i + 1) * HEAD_SIZE)
+            held[:, cols] = got_ref[role * kv_local + i].astype(jnp.float32)
     for i in range(kv_local):
         for role in range(cores):
             mine = (tp * kv_local + i == p) & (tp == role)
@@ -546,55 +584,46 @@
     moves = sum(len(lower(k)) for k in order)
     left(kv_ref.at[0, :, : moves * block, :], kvz_send)
     left(kv_ref.at[0], kvp_send)
-    left(cols_ref.at[:, : half * run, :], x_send, jnp.logical_not(holder))
-    left(cols_ref.at[:, : (half - 1) * run, :], x_send, holder)
-    left(cols_ref, side_send.at[2], holder)
+    left(xs_ref.at[:, : layers * run, :], x_sent, jnp.logical_not(holder))
+    left(xs_ref.at[:, : (layers - 1) * run, :], x_sent, holder)
+    left(xs_ref.at[:, : len(flips) * depth * run, :], xp_send, holder)
+    left(xs_ref, xd_send, holder)
     for i in range(2):
         left(far_ref.at[i], side_send.at[i])
-    left(pair_ref, side_send.at[3])
     left(give_ref, give_send)
     left(take_ref.at[:, : (depth - 1) * block, :], z_send)
     left(dqb_ref, dq_send, guest)
     left(dqb_ref.at[:, :, :fewer, :], dq_send, owner)
-    ways = len(bits)
-    left(sum_all(ways * parts), col_send, owner)
-    left(sum_all((ways + 1) * parts), col_send, guest)
-    left(sum_all((moves - ways) * cores * parts), ag_send.at[0], owner)
-    left(sum_all(depth * cores * parts), ag_send.at[1], owner)
-    left(sum_all(depth * cores * parts), ag_send.at[2], owner)
-    left(sum_all(depth * parts), ag_send.at[3])
+    left(wk_ref.at[:, : moves * block, :], wk_send)
+    left(own_ref.at[: cores * plane - 1], own_sem.at[0])
+    left(out_ref, share_sem.at[0], guest)
+    left(out_ref.at[: plane - 1], share_sem.at[0], owner)
 
 
 def deliver_kernel(*refs):
-    count = (len(refs) - 1) // 3
-    ins, outs, held = refs[:count], refs[count : 2 * count], refs[2 * count : 3 * count]
-    sems = refs[3 * count]
+    count = (len(refs) - 1) // 2
     moves = []
     for i in range(count):
-        moves.append(pltpu.make_async_copy(ins[i], held[i], sems.at[0, i]))
+        moves.append(pltpu.make_async_copy(refs[i], refs[count + i], refs[-1].at[i]))
         moves[-1].start()
-    for i in range(count):
-        moves[i].wait()
-        moves.append(pltpu.make_async_copy(held[i], outs[i], sems.at[1, i]))
-        moves[-1].start()
-    for move in moves[count:]:
+    for move in moves:
         move.wait()
 
 
 def deliver(*arrays):
+    vmem = pl.BlockSpec(memory_space=pltpu.VMEM)
     hbm = pl.BlockSpec(memory_space=pl.ANY)
     count = len(arrays)
     return pl.pallas_call(
         deliver_kernel,
         out_shape=tuple(jax.ShapeDtypeStruct(a.shape, a.dtype) for a in arrays),
-        in_specs=[hbm] * count,
+        in_specs=[vmem] * count,
         out_specs=(hbm,) * count,
-        scratch_shapes=[pltpu.VMEM(a.shape, a.dtype) for a in arrays]
-        + [pltpu.SemaphoreType.DMA((2, count))],
+        scratch_shapes=[pltpu.SemaphoreType.DMA((count,))],
     )(*arrays)
 
 
-def step(n, q, g, k, v, pos, x, km, vm):
+def step(n, q, g, k, v, place, x, km, vm):
     parts, run, width = q.shape
     kv_width = k.shape[2]
     kv_local = kv_width // HEAD_SIZE
@@ -608,7 +637,8 @@
     block = plane * run
     keys = n * run
     wide = pair * block
-    x_width = max(cores * features // n, 128)
+    block_width = cores * features // n
+    x_width = plane * block_width
     roomy = parts * keys <= 4096
     tiles = len(visible(parts, keys))
     vmem = pl.BlockSpec(memory_space=pltpu.VMEM)
@@ -621,11 +651,11 @@
         out_shape=(
             jax.ShapeDtypeStruct((parts, run, width), kind),
             jax.ShapeDtypeStruct((parts * run, features), kind),
-            jax.ShapeDtypeStruct((x_width, kv_width), real),
-            jax.ShapeDtypeStruct((x_width, kv_width), real),
+            jax.ShapeDtypeStruct((block_width, kv_width), real),
+            jax.ShapeDtypeStruct((block_width, kv_width), real),
         ),
-        in_specs=[vmem] * 5 + [hbm] * 3,
-        out_specs=(hbm,) * 4,
+        in_specs=[hbm] * 4 + [vmem] + [hbm] * 3,
+        out_specs=(vmem,) * 4,
         scratch_shapes=[
             pltpu.VMEM((2, parts, keys, HEAD_SIZE), kind),
             pltpu.VMEM((parts, pair, block, HEAD_SIZE), kind),
@@ -641,15 +671,19 @@
             pltpu.VMEM((parts, keys, HEAD_SIZE), kind),
             pltpu.VMEM((parts, keys, HEAD_SIZE), kind),
             pltpu.VMEM((parts, depth - 1, block, HEAD_SIZE), kind),
-            pltpu.VMEM((parts, block, HEAD_SIZE), kind),
-            pltpu.VMEM((parts, 2 * kv_local, keys, HEAD_SIZE), kind),
+            pltpu.VMEM((parts, keys, HEAD_SIZE), kind),
             pltpu.VMEM((parts, keys, x_width), kind),
-            pltpu.VMEM((x_width, 2 * kv_width), real),
-            pltpu.VMEM((parts, 2 * kv_local, run, HEAD_SIZE), kind),
+            pltpu.VMEM((HEAD_SIZE, x_width), real),
+            pltpu.VMEM((cores * plane, parts, run, HEAD_SIZE), kind),
+            pltpu.VMEM((plane, block_width, HEAD_SIZE), kind),
+            pltpu.VMEM((cores * kv_local, block_width, HEAD_SIZE), kind),
             pltpu.VMEM((2, features, kv_width), kind),
             pltpu.VMEM((2, features, kv_width), kind),
             pltpu.VMEM((parts, run, width), kind),
-            pltpu.VMEM((parts * run, features), kind),
+            pltpu.VMEM((parts, run, width), kind),
+            pltpu.VMEM((parts, run, kv_width), kind),
+            pltpu.VMEM((parts, run, kv_width), kind),
+            pltpu.VMEM((depth * parts, block), real),
             dma((kv_local, cores)),
             dma((n,)),
             dma,
@@ -658,38 +692,29 @@
             dma((2,)),
             dma((2,)),
             dma,
-            dma,
-            dma((4,)),
-            dma((4,)),
+            dma((depth,)),
+            dma((2,)),
+            dma((2,)),
             dma((7,)),
             dma,
             dma((parts,)),
             dma,
             dma((parts, levels)),
             dma,
-            dma((4,)),
+            dma((3, depth)),
+            dma,
+            dma,
+            dma,
             dma((parts, depth)),
-            dma((parts, depth)),
-            dma((parts + 1,)),
+            dma((2,)),
+            dma((2,)),
             dma,
             dma,
         ],
         compiler_params=pltpu.CompilerParams(
             vmem_limit_bytes=63 * 2**20, collective_id=0, has_side_effects=True
         ),
-    )(q, g, k, v, pos, x, km, vm)
-
-
-def positions(run_placement, rows_here, parts):
-    seq_count = run_placement.shape[0]
-    run_rows = rows_here // seq_count
-    block = jnp.arange(seq_count, dtype=jnp.int32)[:, None] * rows_here
-    start = jnp.transpose(block + run_placement * run_rows)
-    pos = start[:, :, None] + jnp.arange(run_rows, dtype=jnp.int32)
-    plane = parts
-    pos = pos.reshape(seq_count // plane, plane, parts, rows_here // parts)
-    pos = jnp.transpose(pos, (0, 2, 1, 3)).reshape(seq_count, rows_here)
-    return pos.astype(jnp.float32)
+    )(q, g, k, v, place, x, km, vm)
 
 
 def local(
@@ -706,8 +731,7 @@
     seq_count = run_placement.shape[0]
     rows_here = query_rows.shape[0]
     kv_width = key_rows.shape[1]
-    features = layer_input.shape[1]
-    parts = (key_matrix.shape[0] // features) * (kv_width // HEAD_SIZE)
+    parts = (key_matrix.shape[0] // layer_input.shape[1]) * (kv_width // HEAD_SIZE)
 
     def cut(array):
         return array.reshape(parts, rows_here // parts, array.shape[1])
@@ -718,7 +742,7 @@
         cut(output_grad),
         cut(key_rows),
         cut(stored_value_rows),
-        positions(run_placement, rows_here, parts),
+        run_placement,
         cut(layer_input),
         key_matrix,
         value_matrix,
@@ -726,11 +750,6 @@
     query_grad, input_grad, key_weight, value_weight = deliver(
         query_grad, input_grad, key_weight, value_weight
     )
-    block_width = 2 * features // seq_count
-    if key_weight.shape[0] != block_width:
-        shift = (seq_index * block_width) % key_weight.shape[0]
-        key_weight = lax.dynamic_slice_in_dim(key_weight, shift, block_width, 0)
-        value_weight = lax.dynamic_slice_in_dim(value_weight, shift, block_width, 0)
     return (query_grad.reshape(query_rows.shape), input_grad, key_weight, value_weight)
 
 

time: 74 us -> 63.4 us (0.86)
  the two profiles are of different devices: /device:TPU:7 before, /device:TPU:0 now
where the time goes in v3:
time: 63.4 us; the launch traced here: 63.2 us
  Pallas kernels  62.5 us (99%)
  between operations  0.64 us (1%)
    pallas_call x1, Pallas kernels, step(): pl.pallas_call(step_kernel, out_shape=(jax.ShapeDtypeStruct((parts, run,...  60.2 us
    pallas_call x1, Pallas kernels, deliver(): pl.pallas_call(deliver_kernel, out_shape=tuple((jax.ShapeDtypeStruct(a.sh...  2.35 us

profile of v3, /device:TPU:0, one launch (start us, length us, event | category | flops | bytes accessed | tf_op | source)
XLA Modules:
  0.0 63.2 jit_solution(4216780679750113201)
XLA Ops:
  0.6 60.2 %shard_map.111 = (bf16[4,32,1024]{2,1,0:T(8,128)(2,1)}, bf16[128,2048]{1,0:T(8,128)(2,1)}, f32[256,256]{1,0:T(8,128)}, f32[256,256]{1,0:T(8,128)}) custom-call(bf16[4,32,1024]{2,1,0:T(8,128)(2,1)} %bitcast.7, bf16[4,32,1024]{2,1,0:T(8,128)(2,1)} %bitcast.8, bf16[4,32,256]{2,1,0:T(8,128)(2,1)} %bitcast.9, bf16[4,32,256]{2,1,0:T(8,128)(2,1)} %bitcast.10, ...), custom_call_target="tpu_custom_call" | custom-call | tf_op jit(solution)/shard_map/pallas_call | solution.py:649
  60.8 2.3 %shard_map.112 = (bf16[4,32,1024]{2,1,0:T(8,128)(2,1)}, bf16[128,2048]{1,0:T(8,128)(2,1)}, f32[256,256]{1,0:T(8,128)}, f32[256,256]{1,0:T(8,128)}) custom-call(bf16[4,32,1024]{2,1,0:T(8,128)(2,1)} %get-tuple-element.12.refs_0_, bf16[128,2048]{1,0:T(8,128)(2,1)} %get-tuple-element.13.refs_1_, f32[256,256]{1,0:T(8,128)} %get-tuple-element.14.refs_2_, ...), custom_call_target="tpu_custom_call" | custom-call | tf_op jit(solution)/shard_map/pallas_call | solution.py:617

commit v4 on v3

--- a/solution.py
+++ b/solution.py
@@ -37,10 +37,10 @@
 
 def step_kernel(
     q_in, g_in, k_in, v_in, place_ref, x_ref, km_ref, vm_ref,
-    dq_ref, ig_ref, kw_ref, vw_ref,
+    dq_out, ig_out, kw_out, vw_out,
     kv_ref, qb_ref, gb_ref, kpos_ref, s_ref, dp_ref, p_ref, ds_ref, dqb_ref, dqa_ref,
     sum_ref, give_ref, take_ref, land_ref, wk_ref, xs_ref, acc_ref,
-    own_ref, out_ref, got_ref, near_ref, far_ref, q_ref, g_ref, k_ref, v_ref, pos_ref,
+    own_ref, out_ref, got_ref, near_ref, far_ref, dq_ref, ig_ref, kw_ref, vw_ref, q_ref, g_ref, k_ref, v_ref, pos_ref,
     plane_send, kv_recv, kvz_send, kvp_send, kvp_recv, qg_send, qg_recv,
     x_sent, x_recv, side_send, side_recv, local_sem,
     give_send, give_recv, z_send, z_recv,
@@ -146,10 +146,13 @@
     own_columns = pltpu.make_async_copy(columns_of(z), block_of(me), local_sem.at[2])
     pl.when(holder)(own_columns.start)
 
-    def x_send(slot, early):
-        target = tp * layers + (z + layers - 1 - slot) % layers
+    def x_send(slot, phase):
+        target = jnp.where(tp == 0, layers - 1 - slot, tp * layers + slot)
         clear = (target > z) == (z % 2 == 1)
-        now = clear if early else jnp.logical_not(clear)
+        outer = ((target == 0) | (target == depth - 1)) & (jnp.abs(target - z) > 1)
+        now = outer
+        if phase < 2:
+            now = jnp.logical_not(outer) & (clear if phase == 0 else jnp.logical_not(clear))
         send(
             columns_of(target), block_of(me), x_sent, x_recv.at[z],
             {"seq": target * plane + p, "tp": tp}, (target != z) & now,
@@ -265,7 +268,7 @@
     relayed = [k for k in order if lower(k)]
     pass_on(0)
     for slot in range(layers):
-        x_send(slot, True)
+        x_send(slot, 0)
     for k in relayed[1:]:
         pass_on(k)
 
@@ -279,7 +282,7 @@
         nearby[-1].start()
 
     for slot in range(layers):
-        x_send(slot, False)
+        x_send(slot, 1)
 
     for k in order:
         if k not in relayed:
@@ -303,6 +306,8 @@
             return body(slice(0, keys), carry)
         return lax.fori_loop(0, keys // sub, lambda i, c: body(rows_of(i, sub), c), carry)
 
+    for slot in range(layers):
+        x_send(slot, 2)
     x_relay(0)
     inverse, delta = [], []
     for a in range(parts):
@@ -513,9 +518,16 @@
                 def _():
                     dq_ref[:, :, cols] = dqb_ref[:, h, j * run : (j + 1) * run, :]
 
+    leaving = []
+
+    def put(src, dst):
+        leaving.append(pltpu.make_async_copy(src, dst, local_sem.at[7 + len(leaving)]))
+        leaving[-1].start()
+
     def answers():
         arrive(dqb_ref, dq_recv, guest)
         arrive(dqb_ref.at[:, :, :fewer, :], dq_recv, owner)
+        put(dq_ref, dq_out)
 
     def inputs():
         for copy in nearby:
@@ -536,6 +548,7 @@
             weights = [ref[i, tile, :] for ref in (near_ref, far_ref) for i in range(2)]
             out = dot(grads, jnp.concatenate(weights, axis=1), NT)
             ig_ref[:, tile] = out.astype(jnp.bfloat16)
+        put(ig_ref, ig_out)
 
     last = parts - 1
     for b in reversed(range(parts)):
@@ -555,25 +568,25 @@
                 stage(b)
         if tick == last:
             x_relay(1)
+        if tick == last + len(stages) - 2:
+            own_send()
+            for k in range(2, depth):
+                x_relay(k)
             queries()
-        if tick == last + 1:
-            x_relay(2)
-    for k in range(3, depth):
-        x_relay(k)
-    own_send()
     arrive(xs_ref, xd_recv, jnp.logical_not(holder))
     for b in reversed(range(parts)):
         gather(b)
         weigh(b, b == last)
     share()
+    inputs()
     answers()
-    inputs()
     arrive(got_ref, share_sem.at[1], guest)
     arrive(got_ref.at[: cores * kv_local - 1], share_sem.at[1], owner)
-    for role, held in enumerate((kw_ref, vw_ref)):
+    for role, (held, out) in enumerate(((kw_ref, kw_out), (vw_ref, vw_out))):
         for i in range(kv_local):
             cols = slice(i * HEAD_SIZE, (i + 1) * HEAD_SIZE)
             held[:, cols] = got_ref[role * kv_local + i].astype(jnp.float32)
+        put(held, out)
     for i in range(kv_local):
         for role in range(cores):
             mine = (tp * kv_local + i == p) & (tp == role)
@@ -598,28 +611,35 @@
     left(own_ref.at[: cores * plane - 1], own_sem.at[0])
     left(out_ref, share_sem.at[0], guest)
     left(out_ref.at[: plane - 1], share_sem.at[0], owner)
+    for copy in leaving:
+        copy.wait()
 
 
 def deliver_kernel(*refs):
-    count = (len(refs) - 1) // 2
+    count = (len(refs) - 1) // 3
+    ins, outs, held = refs[:count], refs[count : 2 * count], refs[2 * count : 3 * count]
     moves = []
     for i in range(count):
-        moves.append(pltpu.make_async_copy(refs[i], refs[count + i], refs[-1].at[i]))
+        moves.append(pltpu.make_async_copy(ins[i], held[i], refs[-1].at[0, i]))
         moves[-1].start()
-    for move in moves:
+    for i in range(count):
+        moves[i].wait()
+        moves.append(pltpu.make_async_copy(held[i], outs[i], refs[-1].at[1, i]))
+        moves[-1].start()
+    for move in moves[count:]:
         move.wait()
 
 
 def deliver(*arrays):
-    vmem = pl.BlockSpec(memory_space=pltpu.VMEM)
     hbm = pl.BlockSpec(memory_space=pl.ANY)
     count = len(arrays)
     return pl.pallas_call(
         deliver_kernel,
         out_shape=tuple(jax.ShapeDtypeStruct(a.shape, a.dtype) for a in arrays),
-        in_specs=[vmem] * count,
+        in_specs=[hbm] * count,
         out_specs=(hbm,) * count,
-        scratch_shapes=[pltpu.SemaphoreType.DMA((count,))],
+        scratch_shapes=[pltpu.VMEM(a.shape, a.dtype) for a in arrays]
+        + [pltpu.SemaphoreType.DMA((2, count))],
     )(*arrays)
 
 
@@ -655,7 +675,7 @@
             jax.ShapeDtypeStruct((block_width, kv_width), real),
         ),
         in_specs=[hbm] * 4 + [vmem] + [hbm] * 3,
-        out_specs=(vmem,) * 4,
+        out_specs=(hbm,) * 4,
         scratch_shapes=[
             pltpu.VMEM((2, parts, keys, HEAD_SIZE), kind),
             pltpu.VMEM((parts, pair, block, HEAD_SIZE), kind),
@@ -680,6 +700,10 @@
             pltpu.VMEM((2, features, kv_width), kind),
             pltpu.VMEM((2, features, kv_width), kind),
             pltpu.VMEM((parts, run, width), kind),
+            pltpu.VMEM((parts * run, features), kind),
+            pltpu.VMEM((block_width, kv_width), real),
+            pltpu.VMEM((block_width, kv_width), real),
+            pltpu.VMEM((parts, run, width), kind),
             pltpu.VMEM((parts, run, width), kind),
             pltpu.VMEM((parts, run, kv_width), kind),
             pltpu.VMEM((parts, run, kv_width), kind),
@@ -695,7 +719,7 @@
             dma((depth,)),
             dma((2,)),
             dma((2,)),
-            dma((7,)),
+            dma((11,)),
             dma,
             dma((parts,)),
             dma,

time: 63.4 us -> 60.3 us (0.951)
  Pallas kernels: 62.5 us -> 59.5 us
    pallas_call x1, Pallas kernels: 60.2 us -> 57.3 us  [step(): pl.pallas_call(step_kernel, out_shape=(jax.ShapeDtypeStruct((parts, run,...]
where the time goes in v4:
time: 60.3 us; the launch traced here: 60.1 us
  Pallas kernels  59.5 us (99%)
  between operations  0.64 us (1%)
    pallas_call x1, Pallas kernels, step(): pl.pallas_call(step_kernel, out_shape=(jax.ShapeDtypeStruct((parts, run,...  57.3 us
    pallas_call x1, Pallas kernels, deliver(): pl.pallas_call(deliver_kernel, out_shape=tuple((jax.ShapeDtypeStruct(a.sh...  2.16 us

profile of v4, /device:TPU:0, one launch (start us, length us, event | category | flops | bytes accessed | tf_op | source)
XLA Modules:
  0.0 60.1 jit_solution(13377972770391505828)
XLA Ops:
  0.6 57.3 %shard_map.111 = (bf16[4,32,1024]{2,1,0:T(8,128)(2,1)}, bf16[128,2048]{1,0:T(8,128)(2,1)}, f32[256,256]{1,0:T(8,128)}, f32[256,256]{1,0:T(8,128)}) custom-call(bf16[4,32,1024]{2,1,0:T(8,128)(2,1)} %bitcast.7, bf16[4,32,1024]{2,1,0:T(8,128)(2,1)} %bitcast.8, bf16[4,32,256]{2,1,0:T(8,128)(2,1)} %bitcast.9, bf16[4,32,256]{2,1,0:T(8,128)(2,1)} %bitcast.10, ...), custom_call_target="tpu_custom_call" | custom-call | tf_op jit(solution)/shard_map/pallas_call | solution.py:669
  58.0 2.2 %shard_map.112 = (bf16[4,32,1024]{2,1,0:T(8,128)(2,1)}, bf16[128,2048]{1,0:T(8,128)(2,1)}, f32[256,256]{1,0:T(8,128)}, f32[256,256]{1,0:T(8,128)}) custom-call(bf16[4,32,1024]{2,1,0:T(8,128)(2,1)} %get-tuple-element.12.refs_0_, bf16[128,2048]{1,0:T(8,128)(2,1)} %get-tuple-element.13.refs_1_, f32[256,256]{1,0:T(8,128)} %get-tuple-element.14.refs_2_, ...), custom_call_target="tpu_custom_call" | custom-call | tf_op jit(solution)/shard_map/pallas_call | solution.py:636

commit v5 on v4

--- a/solution.py
+++ b/solution.py
@@ -36,11 +36,11 @@
 
 
 def step_kernel(
-    q_in, g_in, k_in, v_in, place_ref, x_ref, km_ref, vm_ref,
+    q_in, g_in, k_in, v_in, place_in, x_ref, km_ref, vm_ref,
     dq_out, ig_out, kw_out, vw_out,
     kv_ref, qb_ref, gb_ref, kpos_ref, s_ref, dp_ref, p_ref, ds_ref, dqb_ref, dqa_ref,
     sum_ref, give_ref, take_ref, land_ref, wk_ref, xs_ref, acc_ref,
-    own_ref, out_ref, got_ref, near_ref, far_ref, dq_ref, ig_ref, kw_ref, vw_ref, q_ref, g_ref, k_ref, v_ref, pos_ref,
+    own_ref, out_ref, got_ref, near_ref, far_ref, dq_ref, ig_ref, kw_ref, vw_ref, q_ref, g_ref, k_ref, v_ref, pos_ref, place_ref,
     plane_send, kv_recv, kvz_send, kvp_send, kvp_recv, qg_send, qg_recv,
     x_sent, x_recv, side_send, side_recv, local_sem,
     give_send, give_recv, z_send, z_recv,
@@ -139,7 +139,9 @@
         return x_ref.at[:, :, pl.ds(pl.multiple_of(start, x_width), x_width)]
 
     staged = []
-    for src, dst in ((k_in, k_ref), (v_in, v_ref), (q_in, q_ref), (g_in, g_ref)):
+    for src, dst in (
+        (k_in, k_ref), (v_in, v_ref), (q_in, q_ref), (g_in, g_ref), (place_in, place_ref)
+    ):
         staged.append(pltpu.make_async_copy(src, dst, local_sem.at[3 + len(staged)]))
         staged[-1].start()
 
@@ -521,7 +523,7 @@
     leaving = []
 
     def put(src, dst):
-        leaving.append(pltpu.make_async_copy(src, dst, local_sem.at[7 + len(leaving)]))
+        leaving.append(pltpu.make_async_copy(src, dst, local_sem.at[8 + len(leaving)]))
         leaving[-1].start()
 
     def answers():
@@ -557,9 +559,10 @@
             cross(b + 1)
         if b == last - 1:
             x_push(1)
+        if b == 0:
+            for k in range(2, depth):
+                x_push(k)
     cross(0)
-    for k in range(2, depth):
-        x_push(k)
     stages = [fold(e) for e in range(1, len(bits))] + [finish, hand]
     for tick in range(last + len(stages)):
         for level, stage in enumerate(stages):
@@ -661,7 +664,6 @@
     x_width = plane * block_width
     roomy = parts * keys <= 4096
     tiles = len(visible(parts, keys))
-    vmem = pl.BlockSpec(memory_space=pltpu.VMEM)
     hbm = pl.BlockSpec(memory_space=pl.ANY)
     kind = jnp.bfloat16
     real = jnp.float32
@@ -674,7 +676,7 @@
             jax.ShapeDtypeStruct((block_width, kv_width), real),
             jax.ShapeDtypeStruct((block_width, kv_width), real),
         ),
-        in_specs=[hbm] * 4 + [vmem] + [hbm] * 3,
+        in_specs=[hbm] * 8,
         out_specs=(hbm,) * 4,
         scratch_shapes=[
             pltpu.VMEM((2, parts, keys, HEAD_SIZE), kind),
@@ -708,6 +710,7 @@
             pltpu.VMEM((parts, run, kv_width), kind),
             pltpu.VMEM((parts, run, kv_width), kind),
             pltpu.VMEM((depth * parts, block), real),
+            pltpu.VMEM((n, n), jnp.int32),
             dma((kv_local, cores)),
             dma((n,)),
             dma,
@@ -719,7 +722,7 @@
             dma((depth,)),
             dma((2,)),
             dma((2,)),
-            dma((11,)),
+            dma((12,)),
             dma,
             dma((parts,)),
             dma,

time: 60.3 us -> 59.7 us (0.990)
  no operation moved by 1% of the time
where the time goes in v5:
time: 59.7 us; the launch traced here: 59.6 us
  Pallas kernels  58.9 us (99%)
  between operations  0.64 us (1%)
    pallas_call x1, Pallas kernels, step(): pl.pallas_call(step_kernel, out_shape=(jax.ShapeDtypeStruct((parts, run,...  56.8 us
    pallas_call x1, Pallas kernels, deliver(): pl.pallas_call(deliver_kernel, out_shape=tuple((jax.ShapeDtypeStruct(a.sh...  2.16 us

profile of v5, /device:TPU:0, one launch (start us, length us, event | category | flops | bytes accessed | tf_op | source)
XLA Modules:
  0.0 59.6 jit_solution(12921033728396417431)
XLA Ops:
  0.6 56.8 %shard_map.111 = (bf16[4,32,1024]{2,1,0:T(8,128)(2,1)}, bf16[128,2048]{1,0:T(8,128)(2,1)}, f32[256,256]{1,0:T(8,128)}, f32[256,256]{1,0:T(8,128)}) custom-call(bf16[4,32,1024]{2,1,0:T(8,128)(2,1)} %bitcast.7, bf16[4,32,1024]{2,1,0:T(8,128)(2,1)} %bitcast.8, bf16[4,32,256]{2,1,0:T(8,128)(2,1)} %bitcast.9, bf16[4,32,256]{2,1,0:T(8,128)(2,1)} %bitcast.10, ...), custom_call_target="tpu_custom_call" | custom-call | tf_op jit(solution)/shard_map/pallas_call | solution.py:671
  57.4 2.2 %shard_map.112 = (bf16[4,32,1024]{2,1,0:T(8,128)(2,1)}, bf16[128,2048]{1,0:T(8,128)(2,1)}, f32[256,256]{1,0:T(8,128)}, f32[256,256]{1,0:T(8,128)}) custom-call(bf16[4,32,1024]{2,1,0:T(8,128)(2,1)} %get-tuple-element.12.refs_0_, bf16[128,2048]{1,0:T(8,128)(2,1)} %get-tuple-element.13.refs_1_, f32[256,256]{1,0:T(8,128)} %get-tuple-element.14.refs_2_, ...), custom_call_target="tpu_custom_call" | custom-call | tf_op jit(solution)/shard_map/pallas_call | solution.py:639
